TPU v7x, 32 devices: a whole 2x2x4 slice. The times are simulated.
32 devices in a mesh: dp: 4 (over x, core), fsdp: 8 (over z, y).
Axes of the slice: x: 2, y: 2, z: 4, core: 2. Of those that a mesh axis runs over, the one named last changes fastest.
Arguments:
- tokens: bfloat16 [98304, 384], P(('dp', 'fsdp')), may hold values from -3 to 3
- cotangent: bfloat16 [98304, 384], P(('dp', 'fsdp')), may hold values from -6 to 6
- image_start: int32 [98304], P(('dp', 'fsdp')), may hold values from 0 to 98303, as said below
- image_end: int32 [98304], P(('dp', 'fsdp')), may hold values from 1 to 98304, as said below
- qkv_weight: bfloat16 [384, 1152], P(('dp', 'fsdp')), may hold values from -2 to 2
- q_bias: bfloat16 [384], P(('dp', 'fsdp')), may hold values from -3 to 3
- v_bias: bfloat16 [384], P(('dp', 'fsdp')), may hold values from -3 to 3
- out_weight: bfloat16 [384, 384], P(('dp', 'fsdp')), may hold values from -4 to 4
- out_bias: bfloat16 [384], P(('dp', 'fsdp')), may hold values from -3 to 3
- up_weight: bfloat16 [384, 1536], P(('dp', 'fsdp')), may hold values from -0.3125 to 0.3125
- up_bias: bfloat16 [1536], P(('dp', 'fsdp')), may hold values from -3 to 3
- down_weight: bfloat16 [1536, 384], P(('dp', 'fsdp')), may hold values from -0.15625 to 0.15625
- down_bias: bfloat16 [384], P(('dp', 'fsdp')), may hold values from -3 to 3
- first_gain: bfloat16 [384], P(('dp', 'fsdp')), may hold values from 0.099609375 to 1.8984375
- first_bias: bfloat16 [384], P(('dp', 'fsdp')), may hold values from -3 to 3
- second_gain: bfloat16 [384], P(('dp', 'fsdp')), may hold values from 0.099609375 to 1.8984375
- second_bias: bfloat16 [384], P(('dp', 'fsdp')), may hold values from -3 to 3
Outputs:
- layer_out: bfloat16 [98304, 384], P(('dp', 'fsdp'))
- input_token_gradient: float32 [98304, 384], P(('dp', 'fsdp'))
- qkv_weight_grad: float32 [384, 1152], P(('dp', 'fsdp'))
- q_bias_grad: float32 [384], P(('dp', 'fsdp'))
- v_bias_grad: float32 [384], P(('dp', 'fsdp'))
- out_weight_grad: float32 [384, 384], P(('dp', 'fsdp'))
- out_bias_grad: float32 [384], P(('dp', 'fsdp'))
- up_weight_grad: float32 [384, 1536], P(('dp', 'fsdp'))
- up_bias_grad: float32 [1536], P(('dp', 'fsdp'))
- down_weight_grad: float32 [1536, 384], P(('dp', 'fsdp'))
- down_bias_grad: float32 [384], P(('dp', 'fsdp'))
- first_gain_grad: float32 [384], P(('dp', 'fsdp'))
- first_bias_grad: float32 [384], P(('dp', 'fsdp'))
- second_gain_grad: float32 [384], P(('dp', 'fsdp'))
- second_bias_grad: float32 [384], P(('dp', 'fsdp'))
Inputs may be any that keep to these rules, and one draw needn't show every extreme that they name: Images are runs of consecutive tokens of 98 to 197 tokens each; every boundary between the tokens of two devices (multiples of 3072 inside the stream) lies inside an image of exactly 197 tokens, of which 197 // 4 to 98 lie below the boundary; no other image crosses such a boundary; image_start[t] <= t < image_end[t], and all tokens of an image carry the same two values. `image_end`: see image_start.
All inputs are finite; a program needn't handle non-finite values.
Results may differ from a plain program's by a relative error of at most 0.012.
Values may be sent and summed in bfloat16 or wider, within the bound.
A program may use at most 448 MiB of HBM per device.

v0:
```python
import math

import jax
import jax.numpy as jnp
from jax import lax
from jax.sharding import PartitionSpec as P

HEADS = 6
HDIM = 64
RIM = 256


epsilon = 1e-06
masked_score = -1e30
root_half = 0.7071067811865476
gauss_norm = 0.3989422804014327


def padded_2(cells, sides, width):
    for axis, dim in sides:
        count = lax.axis_size(axis)
        ends = count - 1
        head = lax.slice_in_dim(cells, 0, width, axis=dim)
        tail = lax.slice_in_dim(cells, cells.shape[dim] - width, cells.shape[dim], axis=dim)
        cells = jnp.concatenate(
            [
                lax.ppermute(tail, axis, [(i, (i + 1) % count) for i in range(ends)]),
                cells,
                lax.ppermute(head, axis, [((i + 1) % count, i) for i in range(ends)]),
            ],
            axis=dim,
        )
    return cells


def passed_along(value, axis, steps):
    count = lax.axis_size(axis)
    leading, last = (max(0, -steps), min(count, count - steps))
    return lax.ppermute(value, axis, [(source, source + steps) for source in range(leading, last)])


def row_layer_norm(rows, gain, shift):
    centre = rows - jnp.mean(rows, axis=-1, keepdims=True)
    inverse = lax.rsqrt(jnp.mean(centre * centre, axis=-1, keepdims=True) + epsilon)
    normed = centre * inverse
    return (normed * gain + shift, normed, inverse)


def norm_reverse_pass(grad, normed, inverse, gain):
    scaled = grad * gain
    return inverse * (
        scaled
        - jnp.mean(scaled, axis=-1, keepdims=True)
        - normed * jnp.mean(scaled * normed, axis=-1, keepdims=True)
    )


def gelu_value(pre):
    return 0.5 * pre * (1.0 + lax.erf(pre * root_half))


def gelu_slope(pre):
    return 0.5 * (1.0 + lax.erf(pre * root_half)) + pre * jnp.exp(-0.5 * pre * pre) * gauss_norm


def inner_rows(left, right):
    return jnp.dot(left.T, right, preferred_element_type=jnp.float32)


def back_product(left, weight):
    return jnp.dot(left, weight.T, preferred_element_type=jnp.float32)


def block_scores(queries, keys, first_key, end_key, key_pos):
    scores = jnp.einsum("qhd,khd->hqk", queries, keys, preferred_element_type=jnp.float32)
    inside = (key_pos[None, :] >= first_key[:, None]) & (key_pos[None, :] < end_key[:, None])
    return jnp.where(inside[None], scores, masked_score)


def per_device(
    tokens,
    cotangent,
    image_start,
    image_end,
    qkv_weight,
    q_bias,
    v_bias,
    out_weight,
    out_bias,
    up_weight,
    up_bias,
    down_weight,
    down_bias,
    first_gain,
    first_bias,
    second_gain,
    second_bias,
):
    single_precision = jnp.float32
    bf16 = jnp.bfloat16
    rows = tokens.shape[0]
    width = tokens.shape[1]
    rim = RIM
    block = min(512, rows)
    scale = 1.0 / math.sqrt(HDIM)
    params = (
        qkv_weight,
        q_bias,
        v_bias,
        out_weight,
        out_bias,
        up_weight,
        up_bias,
        down_weight,
        down_bias,
        first_gain,
        first_bias,
        second_gain,
        second_bias,
    )
    gathered = (
        lax.all_gather(params[0], ("dp", "fsdp"), axis=0, tiled=True),
        lax.all_gather(params[1], ("dp", "fsdp"), axis=0, tiled=True),
        lax.all_gather(params[2], ("dp", "fsdp"), axis=0, tiled=True),
        lax.all_gather(params[3], ("dp", "fsdp"), axis=0, tiled=True),
        lax.all_gather(params[4], ("dp", "fsdp"), axis=0, tiled=True),
        lax.all_gather(params[5], ("dp", "fsdp"), axis=0, tiled=True),
        lax.all_gather(params[6], ("dp", "fsdp"), axis=0, tiled=True),
        lax.all_gather(params[7], ("dp", "fsdp"), axis=0, tiled=True),
        lax.all_gather(params[8], ("dp", "fsdp"), axis=0, tiled=True),
        lax.all_gather(params[9], ("dp", "fsdp"), axis=0, tiled=True),
        lax.all_gather(params[10], ("dp", "fsdp"), axis=0, tiled=True),
        lax.all_gather(params[11], ("dp", "fsdp"), axis=0, tiled=True),
        lax.all_gather(params[12], ("dp", "fsdp"), axis=0, tiled=True),
    )
    (
        w_qkv,
        b_query,
        b_value,
        w_out,
        b_out,
        w_up,
        b_up,
        w_down,
        b_down,
        leading_gain,
        leading_bias,
        trailing_gain,
        trailing_bias,
    ) = gathered
    leading_gain = leading_gain.astype(single_precision)
    leading_bias = leading_bias.astype(single_precision)
    trailing_gain = trailing_gain.astype(single_precision)
    trailing_bias = trailing_bias.astype(single_precision)
    value_shift = jnp.concatenate(
        [jnp.zeros((width,), single_precision), b_value.astype(single_precision)]
    )
    base = lax.axis_index(("dp", "fsdp")) * rows
    token_row_matrix = tokens.astype(single_precision)
    first_normalized, first_centred_scaled, first_inverse_std = row_layer_norm(
        token_row_matrix, leading_gain, leading_bias
    )
    n1 = first_normalized.astype(bf16)
    qkv = jnp.dot(n1, w_qkv, preferred_element_type=single_precision)
    queries = ((qkv[:, :width] + b_query.astype(single_precision)) * scale).astype(bf16)
    key_vals = (qkv[:, width:] + value_shift).astype(bf16)
    padded = padded_2(key_vals, ((("dp", "fsdp"), 0),), rim)
    key_pos = base - rim + jnp.arange(rows + 2 * rim)
    outs = []
    totals = []
    for idx in range(rows // block):
        low = idx * block
        q_blk = queries[low : low + block].reshape(block, HEADS, HDIM)
        span = padded[low : low + block + 2 * rim]
        keys = span[:, :width].reshape(-1, HEADS, HDIM)
        values = span[:, width:].reshape(-1, HEADS, HDIM)
        scores = block_scores(
            q_blk,
            keys,
            image_start[low : low + block],
            image_end[low : low + block],
            key_pos[low : low + block + 2 * rim],
        )
        top = jnp.max(scores, axis=-1, keepdims=True)
        lse = top + jnp.log(jnp.sum(jnp.exp(scores - top), axis=-1, keepdims=True))
        probs_b = jnp.exp(scores - lse).astype(bf16)
        out = jnp.einsum("hqk,khd->qhd", probs_b, values, preferred_element_type=single_precision)
        outs.append(out.reshape(block, width).astype(bf16))
        totals.append(lse)
    attended = jnp.concatenate(outs, axis=0)
    hidden_state = (
        token_row_matrix
        + jnp.dot(attended, w_out, preferred_element_type=single_precision)
        + b_out.astype(single_precision)
    )
    second_normalized, second_centred_scaled, second_inverse_std = row_layer_norm(
        hidden_state, trailing_gain, trailing_bias
    )
    n2 = second_normalized.astype(bf16)
    pre = jnp.dot(n2, w_up, preferred_element_type=single_precision) + b_up.astype(single_precision)
    act = gelu_value(pre).astype(bf16)
    layer_out = (
        hidden_state
        + jnp.dot(act, w_down, preferred_element_type=single_precision)
        + b_down.astype(single_precision)
    ).astype(bf16)
    backward_set = (
        lax.all_gather(params[0], ("dp", "fsdp"), axis=0, tiled=True),
        lax.all_gather(params[1], ("dp", "fsdp"), axis=0, tiled=True),
        lax.all_gather(params[2], ("dp", "fsdp"), axis=0, tiled=True),
        lax.all_gather(params[3], ("dp", "fsdp"), axis=0, tiled=True),
        lax.all_gather(params[4], ("dp", "fsdp"), axis=0, tiled=True),
        lax.all_gather(params[5], ("dp", "fsdp"), axis=0, tiled=True),
        lax.all_gather(params[6], ("dp", "fsdp"), axis=0, tiled=True),
        lax.all_gather(params[7], ("dp", "fsdp"), axis=0, tiled=True),
        lax.all_gather(params[8], ("dp", "fsdp"), axis=0, tiled=True),
        lax.all_gather(params[9], ("dp", "fsdp"), axis=0, tiled=True),
        lax.all_gather(params[10], ("dp", "fsdp"), axis=0, tiled=True),
        lax.all_gather(params[11], ("dp", "fsdp"), axis=0, tiled=True),
        lax.all_gather(params[12], ("dp", "fsdp"), axis=0, tiled=True),
    )
    back_qkv = backward_set[0]
    back_out = backward_set[3]
    back_up = backward_set[5]
    back_down = backward_set[7]
    gradient_function = cotangent.astype(single_precision)
    g_down = inner_rows(act, cotangent)
    g_bdown = jnp.sum(gradient_function, axis=0)
    d_pre = back_product(cotangent, back_down) * gelu_slope(pre)
    d_pre_b = d_pre.astype(bf16)
    g_up = inner_rows(n2, d_pre_b)
    g_bup = jnp.sum(d_pre, axis=0)
    second_normed_grad = back_product(d_pre_b, back_up)
    trailing_gain_grad = jnp.sum(second_normed_grad * second_centred_scaled, axis=0)
    g_bias2 = jnp.sum(second_normed_grad, axis=0)
    hidden_layer_grad = gradient_function + norm_reverse_pass(
        second_normed_grad, second_centred_scaled, second_inverse_std, trailing_gain
    )
    d_hid_b = hidden_layer_grad.astype(bf16)
    g_out = inner_rows(attended, d_hid_b)
    g_bout = jnp.sum(hidden_layer_grad, axis=0)
    d_att = back_product(d_hid_b, back_out).astype(bf16)
    key_grad = jnp.zeros((rows + 2 * rim, width), single_precision)
    value_grad = jnp.zeros((rows + 2 * rim, width), single_precision)
    query_grads = []
    for idx in range(rows // block):
        low = idx * block
        q_blk = queries[low : low + block].reshape(block, HEADS, HDIM)
        span = padded[low : low + block + 2 * rim]
        keys = span[:, :width].reshape(-1, HEADS, HDIM)
        values = span[:, width:].reshape(-1, HEADS, HDIM)
        scores = block_scores(
            q_blk,
            keys,
            image_start[low : low + block],
            image_end[low : low + block],
            key_pos[low : low + block + 2 * rim],
        )
        probs = jnp.exp(scores - totals[idx])
        probs_b = probs.astype(bf16)
        d_out = d_att[low : low + block].reshape(block, HEADS, HDIM)
        value_part = jnp.einsum(
            "hqk,qhd->khd", probs_b, d_out, preferred_element_type=single_precision
        )
        d_probs = jnp.einsum("qhd,khd->hqk", d_out, values, preferred_element_type=single_precision)
        d_scores = (probs * (d_probs - jnp.sum(probs * d_probs, axis=-1, keepdims=True))).astype(
            bf16
        )
        query_part = jnp.einsum(
            "hqk,khd->qhd", d_scores, keys, preferred_element_type=single_precision
        )
        key_part = jnp.einsum(
            "hqk,qhd->khd", d_scores, q_blk, preferred_element_type=single_precision
        )
        key_grad = key_grad.at[low : low + block + 2 * rim].add(key_part.reshape(-1, width))
        value_grad = value_grad.at[low : low + block + 2 * rim].add(value_part.reshape(-1, width))
        query_grads.append(query_part.reshape(block, width))
    kv_grad = jnp.concatenate([key_grad, value_grad], axis=1)
    from_next = passed_along(kv_grad[:rim], ("dp", "fsdp"), -1)
    from_prev = passed_along(kv_grad[rows + rim :], ("dp", "fsdp"), 1)
    own = kv_grad[rim : rim + rows]
    own = own.at[:rim].add(from_prev)
    own = own.at[rows - rim :].add(from_next)
    d_q = jnp.concatenate(query_grads, axis=0) * scale
    d_qkv = jnp.concatenate([d_q, own], axis=1).astype(bf16)
    g_qkv = inner_rows(n1, d_qkv)
    g_bq = jnp.sum(d_q, axis=0)
    g_bv = jnp.sum(own[:, width:], axis=0)
    first_normed_grad = back_product(d_qkv, back_qkv)
    leading_gain_grad = jnp.sum(first_normed_grad * first_centred_scaled, axis=0)
    g_bias1 = jnp.sum(first_normed_grad, axis=0)
    input_token_gradient = hidden_layer_grad + norm_reverse_pass(
        first_normed_grad, first_centred_scaled, first_inverse_std, leading_gain
    )
    partial_sums = (
        lax.psum_scatter(g_qkv, "dp", scatter_dimension=0, tiled=True),
        lax.psum_scatter(g_bq, "dp", scatter_dimension=0, tiled=True),
        lax.psum_scatter(g_bv, "dp", scatter_dimension=0, tiled=True),
        lax.psum_scatter(g_out, "dp", scatter_dimension=0, tiled=True),
        lax.psum_scatter(g_bout, "dp", scatter_dimension=0, tiled=True),
        lax.psum_scatter(g_up, "dp", scatter_dimension=0, tiled=True),
        lax.psum_scatter(g_bup, "dp", scatter_dimension=0, tiled=True),
        lax.psum_scatter(g_down, "dp", scatter_dimension=0, tiled=True),
        lax.psum_scatter(g_bdown, "dp", scatter_dimension=0, tiled=True),
        lax.psum_scatter(leading_gain_grad, "dp", scatter_dimension=0, tiled=True),
        lax.psum_scatter(g_bias1, "dp", scatter_dimension=0, tiled=True),
        lax.psum_scatter(trailing_gain_grad, "dp", scatter_dimension=0, tiled=True),
        lax.psum_scatter(g_bias2, "dp", scatter_dimension=0, tiled=True),
    )
    shards = lax.psum_scatter(tuple(partial_sums), "fsdp", scatter_dimension=0, tiled=True)
    return (layer_out, input_token_gradient) + tuple(shards)


def solution(mesh):
    in_specs = (
        P(("dp", "fsdp"), None),
        P(("dp", "fsdp"), None),
        P(("dp", "fsdp")),
        P(("dp", "fsdp")),
        P(("dp", "fsdp"), None),
        P(("dp", "fsdp")),
        P(("dp", "fsdp")),
        P(("dp", "fsdp"), None),
        P(("dp", "fsdp")),
        P(("dp", "fsdp"), None),
        P(("dp", "fsdp")),
        P(("dp", "fsdp"), None),
        P(("dp", "fsdp")),
        P(("dp", "fsdp")),
        P(("dp", "fsdp")),
        P(("dp", "fsdp")),
        P(("dp", "fsdp")),
    )
    out_specs = (
        P(("dp", "fsdp"), None),
        P(("dp", "fsdp"), None),
        P(("dp", "fsdp"), None),
        P(("dp", "fsdp")),
        P(("dp", "fsdp")),
        P(("dp", "fsdp"), None),
        P(("dp", "fsdp")),
        P(("dp", "fsdp"), None),
        P(("dp", "fsdp")),
        P(("dp", "fsdp"), None),
        P(("dp", "fsdp")),
        P(("dp", "fsdp")),
        P(("dp", "fsdp")),
        P(("dp", "fsdp")),
        P(("dp", "fsdp")),
    )
    return jax.shard_map(
        per_device, mesh=mesh, in_specs=in_specs, out_specs=out_specs, check_vma=False
    )
```

profile of v0, /device:TPU:0, one launch (start us, length us, event | category | flops | bytes accessed | tf_op | source)
XLA Modules:
  0.0 843.6 jit_solution(14169488444738335464)
XLA Ops:
  15.6 42.3 %all-reduce.38 = (bf16[384]{0:T(512)(128)(2,1)S(1)}, bf16[384]{0:T(512)(128)(2,1)S(1)}, bf16[384]{0:T(512)(128)(2,1)S(1)}, bf16[384]{0:T(512)(128)(2,1)S(1)}, bf...) all-reduce(bf16[384]{0:T(512)(128)(2,1)S(1)} %dynamic-update-slice., ...), channel_id=1, replica_groups=mesh['dp'=4,'fsdp'=8] {'dp','fsdp'}, use_global_device_ids=true, to_apply=%add.4 | all-reduce | flops 4608 | bytes 18432
  57.9 74.4 %all-gather = bf16[32,12,1152]{2,1,0:T(8,128)(2,1)S(1)} all-gather(bf16[1,12,1152]{2,1,0:T(8,128)(2,1)} %bitcast.297), channel_id=1, replica_groups=mesh['dp'=4,'fsdp'=8] {'dp','fsdp'}, dimensions={0}, use_global_device_ids=true | all-gather | bytes 912384 | tf_op jit(solution)/shard_map/all_gather | solution.py:122
  138.2 8.5 %fusion.92 = f32[3072,1152]{0,1:T(8,128)} fusion(bf16[384,1152]{1,0:T(8,128)(2,1)} %reshape.993, bf16[3072,384]{0,1:T(8,128)(2,1)S(1)} %copy.50, f32[384]{0:T(512)S(1)} %convert_element_type.157, f32[384]{0:T(512)S(1)} %convert_element_type.156, f32[3072]{0:T(1024)S(1)} %add_rsqrt_fusion.1, f32[3072]{0:T(1024)S(1)} %broadcast_multiply_fusion.5), kind=kOutput, calls=%fused_computation.194 | convolution fusion | flops 2724986880 | bytes 17427456 | tf_op jit(solution)/shard_map/dot_general | solution.py:164
  169.7 70.9 %all-gather.1 = bf16[32,12,384]{2,1,0:T(8,128)(2,1)} all-gather(bf16[1,12,384]{2,1,0:T(8,128)(2,1)S(1)} %bitcast.298), channel_id=1, replica_groups=mesh['dp'=4,'fsdp'=8] {'dp','fsdp'}, dimensions={0}, use_global_device_ids=true | all-gather | bytes 304128 | tf_op jit(solution)/shard_map/all_gather | solution.py:125
  309.5 8.6 %convolution_convert_fusion.2 = bf16[6,64,512]{2,1,0:T(8,128)(2,1)} fusion(bf16[1024,6,64]{0,2,1:T(8,128)(2,1)} %bitcast.274, f32[6,512,1024]{2,1,0:T(8,128)} %copy-done.1, f32[6,512]{1,0:T(8,128)S(1)} %log_add_fusion.1, pred[512,1024]{1,0:T(8,128)(4,1)} %get-tuple-element.357), kind=kOutput, calls=%fused_computation.124 | convolution fusion | flops 412286976 | bytes 14299136 | tf_op jit(solution)/shard_map/hqk,khd->qhd/dot_general | solution.py:187
  342.5 14.0 %multiply_convert_fusion = (bf16[3072,1536]{1,0:T(8,128)(2,1)}, f32[3072,1536]{1,0:T(8,128)}) fusion(f32[1536]{0:T(1024)S(1)} %copy-done.113, bf16[384,1536]{1,0:T(8,128)(2,1)} %reshape.997, f32[3072,384]{0,1:T(8,128)} %copy-done.10, f32[384]{0:T(512)S(1)} %copy-done.117, f32[384]{0:T(512)S(1)} %convert_element_type.187, f32[3072]{0:T(1024)S(1)} %add_rsqrt_fusion, ...), kind=kOutput, calls=%fused_computation.6 | convolution fusion | flops 3658088448 | bytes 34243584 | tf_op jit(solution)/shard_map/dot_general | solution.py:200
  356.5 16.2 %fusion.105 = (f32[1536]{0:T(1024)}, bf16[3072,1536]{1,0:T(8,128)(2,1)S(1)}) fusion(f32[3072,1536]{1,0:T(8,128)} %get-tuple-element.337, f32[1536]{0:T(1024)S(1)} %copy-done.113, bf16[3072,384]{1,0:T(8,128)(2,1)S(1)} %copy-done.78, bf16[1536,384]{1,0:T(8,128)(2,1)} %all-gather.6.cloned.1.call-done), kind=kOutput, calls=%fused_computation.205 | convolution fusion | flops 3680500224 | bytes 31862784 | tf_op jit(solution)/shard_map/dot_general | solution.py:71
  406.4 8.4 multiply_reduce_fusion.5
  420.0 8.1 multiply_reduce_fusion.4
  433.4 8.2 multiply_reduce_fusion.3
  445.8 8.1 multiply_reduce_fusion.2
  464.7 9.2 %fusion.120 = f32[1536,384]{1,0:T(8,128)} fusion(bf16[3072,1536]{1,0:T(8,128)(2,1)} %get-tuple-element.336, bf16[3072,384]{1,0:T(8,128)(2,1)S(1)} %copy-done.79), kind=kOutput, calls=%fused_computation.220 | convolution fusion | flops 3623878656 | bytes 14155776 | tf_op jit(solution)/shard_map/dot_general | solution.py:67
  482.0 10.0 %multiply_convert_fusion.6 = bf16[6,512,1024]{2,1,0:T(8,128)(2,1)S(1)} fusion(f32[6,512,1024]{2,1,0:T(8,128)} %get-tuple-element.339, f32[6,512,1024]{2,1,0:T(8,128)} %copy-done.3, f32[6,512]{1,0:T(8,128)S(1)} %get-tuple-element.338, f32[6,512]{1,0:T(8,128)S(1)} %copy-done.89, pred[512,1024]{1,0:T(8,128)(4,1)S(1)} %copy-done.33), kind=kLoop, calls=%fused_computation.24 | loop fusion | flops 15728640 | bytes 32006144 | tf_op jit(solution)/shard_map/convert_element_type | solution.py:266
  504.0 10.6 %multiply_convert_fusion.5 = bf16[6,512,1024]{2,1,0:T(8,128)(2,1)} fusion(f32[6,512,1024]{2,1,0:T(8,128)} %get-tuple-element.341, f32[6,512,1024]{2,1,0:T(8,128)S(1)} %bitcast.207, f32[6,512]{1,0:T(8,128)S(1)} %get-tuple-element.340, f32[6,512]{1,0:T(8,128)S(1)} %copy-done.92, pred[512,1024]{1,0:T(8,128)(4,1)} %copy-done.28), kind=kLoop, calls=%fused_computation.22 | loop fusion | flops 15728640 | bytes 32006144 | tf_op jit(solution)/shard_map/convert_element_type | solution.py:266
  519.9 10.5 %multiply_convert_fusion.4 = bf16[6,512,1024]{2,1,0:T(8,128)(2,1)} fusion(f32[6,512,1024]{2,1,0:T(8,128)} %get-tuple-element.343, f32[6,512,1024]{2,1,0:T(8,128)S(1)} %bitcast.201, f32[6,512]{1,0:T(8,128)S(1)} %get-tuple-element.342, f32[6,512]{1,0:T(8,128)S(1)} %copy-done.90, pred[512,1024]{1,0:T(8,128)(4,1)} %get-tuple-element.359), kind=kLoop, calls=%fused_computation.20 | loop fusion | flops 15728640 | bytes 32006144 | tf_op jit(solution)/shard_map/convert_element_type | solution.py:266
  535.8 10.4 %multiply_convert_fusion.3 = bf16[6,512,1024]{2,1,0:T(8,128)(2,1)} fusion(f32[6,512,1024]{2,1,0:T(8,128)} %get-tuple-element.345, f32[6,512,1024]{2,1,0:T(8,128)S(1)} %bitcast.195, f32[6,512]{1,0:T(8,128)S(1)} %get-tuple-element.344, f32[6,512]{1,0:T(8,128)S(1)} %copy-done.87, pred[512,1024]{1,0:T(8,128)(4,1)S(1)} %copy-done.25), kind=kLoop, calls=%fused_computation.18 | loop fusion | flops 15728640 | bytes 32006144 | tf_op jit(solution)/shard_map/convert_element_type | solution.py:266
  551.6 10.0 %multiply_convert_fusion.2 = bf16[6,512,1024]{2,1,0:T(8,128)(2,1)} fusion(f32[6,512,1024]{2,1,0:T(8,128)} %get-tuple-element.347, f32[6,512,1024]{2,1,0:T(8,128)S(1)} %bitcast.189, f32[6,512]{1,0:T(8,128)S(1)} %get-tuple-element.346, f32[6,512]{1,0:T(8,128)S(1)} %log_add_fusion.1, pred[512,1024]{1,0:T(8,128)(4,1)S(1)} %copy-done.23), kind=kLoop, calls=%fused_computation.16 | loop fusion | flops 15728640 | bytes 32006144 | tf_op jit(solution)/shard_map/convert_element_type | solution.py:266
  584.4 9.5 %multiply_convert_fusion.1 = bf16[6,512,1024]{2,1,0:T(8,128)(2,1)} fusion(f32[6,512,1024]{2,1,0:T(8,128)} %get-tuple-element.349, f32[6,512,1024]{2,1,0:T(8,128)S(1)} %bitcast.185, f32[6,512]{1,0:T(8,128)S(1)} %get-tuple-element.348, f32[6,512]{1,0:T(8,128)S(1)} %copy-done.86, pred[512,1024]{1,0:T(8,128)(4,1)S(1)} %copy-done.21), kind=kLoop, calls=%fused_computation.14 | loop fusion | flops 15728640 | bytes 32006144 | tf_op jit(solution)/shard_map/convert_element_type | solution.py:266
  622.6 10.5 %fusion.33 = f32[384,1536]{1,0:T(8,128)} fusion(bf16[3072,1536]{1,0:T(8,128)(2,1)} %copy-done.122, f32[3072,384]{0,1:T(8,128)} %copy-done.10, f32[384]{0:T(512)S(1)} %copy-done.118, f32[384]{0:T(512)S(1)} %copy-done.104, f32[3072]{0:T(1024)S(1)} %copy-done.100, f32[3072]{0:T(1024)S(1)} %copy-done.96), kind=kOutput, calls=%fused_computation.80 | convolution fusion | flops 3629776896 | bytes 16542720 | tf_op jit(solution)/shard_map/dot_general | solution.py:67
  689.9 11.1 %add_convert_fusion = bf16[3072,384]{0,1:T(8,128)(2,1)} fusion(f32[3072,384]{0,1:T(8,128)} %copy-done.10, bf16[3072,1536]{1,0:T(8,128)(2,1)} %get-tuple-element.336, bf16[1536,384]{1,0:T(8,128)(2,1)} %all-gather.6.cloned.1.call-done, f32[384]{0:T(512)S(1)} %convert_element_type.192), kind=kOutput, calls=%fused_computation.84 | convolution fusion | flops 3627417600 | bytes 17696256 | tf_op jit(solution)/shard_map/dot_general | solution.py:204
  705.5 9.6 %fusion.106 = (f32[384]{0:T(512)S(1)}, f32[3072,384]{1,0:T(8,128)}) fusion(bf16[384,1152]{1,0:T(8,128)(2,1)S(1)} %copy-done.81, bf16[3072,768]{0,1:T(8,128)(2,1)} %copy-done.58, bf16[3072,384]{0,1:T(8,128)(2,1)} %get-tuple-element.276), kind=kOutput, calls=%fused_computation.206 | convolution fusion | flops 2733243904 | bytes 12682752 | tf_op jit(solution)/shard_map/dot_general | solution.py:71
  733.3 39.1 %fusion.95 = (f32[16,1152]{1,0:T(8,128)S(1)}, f32[16,384]{1,0:T(8,128)S(1)}, f32[16,1536]{1,0:T(8,128)S(1)}) fusion(f32[96,1152]{1,0:T(8,128)} %reduce-scatter.12.cloned.1.call-done, f32[96,384]{1,0:T(8,128)} %reduce-scatter.14.cloned.1.call-done, f32[96,1536]{1,0:T(8,128)} %reduce-scatter.16.cloned.1.call-done), kind=kCustom, calls=%all-reduce-scatter.3 | all-reduce-scatter fusion | flops 393217 | bytes 1376768
  778.0 13.8 %all-reduce.37 = (f32[384]{0:T(512)S(1)}, f32[384]{0:T(512)S(1)}, f32[384]{0:T(512)S(1)}, f32[1536]{0:T(1024)S(1)}, f32[384]{0:T(512)S(1)}, /*index=5*/f32[384]{...) all-reduce(f32[384]{0:T(512)S(1)} %get-tuple-element.275, ...), channel_id=4, replica_groups=mesh['dp'=4,'fsdp'=8] {'dp'}, use_global_device_ids=true, to_apply=%region_29.30.clone | all-reduce | flops 4608 | bytes 36864
  792.5 20.3 %all-reduce.36 = (f32[96]{0:T(128)S(1)}, f32[96]{0:T(128)S(1)}, f32[96]{0:T(128)S(1)}, f32[384]{0:T(512)S(1)}, f32[96]{0:T(128)S(1)}, /*index=5*/f32[96]{0:T(128...) all-reduce(f32[96]{0:T(128)S(1)} %dynamic-slice.101, ...), channel_id=5, replica_groups=mesh['dp'=4,'fsdp'=8] {'fsdp'}, use_global_device_ids=true, to_apply=%region_30.31.clone | all-reduce | flops 1152 | bytes 9216
  (578 shorter events, 381.2 us)
Async XLA Ops:
  7.2 332.3 %all-gather.8.cloned.1.call-start = ((), (), s32[]{:S(2)}) async-start(), calls=%async_computation.11 | async-start | bytes 1622016 | tf_op jit(solution)/shard_map/all_gather | solution.py:127
  7.9 348.6 %all-gather.6.cloned.1.call-start = ((), (), s32[]{:S(2)}) async-start(), calls=%async_computation.5 | async-start | bytes 1216512 | tf_op jit(solution)/shard_map/all_gather | solution.py:129
  57.9 79.5 %copy-start.115 = (f32[384]{0:T(512)}, f32[384]{0:T(512)S(1)}, u32[]{:S(2)}) copy-start(f32[384]{0:T(512)S(1)} %convert_element_type.157) | copy-start | bytes 4612
  57.9 79.5 %copy-start.101 = (f32[384]{0:T(512)}, f32[384]{0:T(512)S(1)}, u32[]{:S(2)}) copy-start(f32[384]{0:T(512)S(1)} %convert_element_type.156) | copy-start | bytes 4612
  136.2 198.6 %copy-start.8 = (bf16[3072,384]{0,1:T(8,128)(2,1)}, bf16[3072,384]{0,1:T(8,128)(2,1)S(1)}, u32[]{:S(2)}) copy-start(bf16[3072,384]{0,1:T(8,128)(2,1)S(1)} %copy.50) | copy-start | bytes 7077892
  155.0 93.6 %collective-permute-start.1 = (bf16[256,768]{0,1:T(8,128)(2,1)}, bf16[256,768]{0,1:T(8,128)(2,1)}, u32[]{:S(2)}, u32[]{:S(2)}) collective-permute-start(bf16[256,768]{0,1:T(8,128)(2,1)} %get-tuple-element.287), channel_id=1, source_target_pairs={{1,0},{2,1},{3,2},{4,3},{5,4},{6,5},{7,6},{8,7},{9,8},{10,9},{11,1... | collective-permute-start | bytes 1179656 | tf_op jit(solution)/shard_map/ppermute | solution.py:29
  156.3 92.4 %collective-permute-start = (bf16[256,768]{0,1:T(8,128)(2,1)}, bf16[256,768]{0,1:T(8,128)(2,1)}, u32[]{:S(2)}, u32[]{:S(2)}) collective-permute-start(bf16[256,768]{0,1:T(8,128)(2,1)} %get-tuple-element.288), channel_id=1, source_target_pairs={{0,1},{1,2},{2,3},{3,4},{4,5},{5,6},{6,7},{7,8},{8,9},{9,10},{10,1... | collective-permute-start | bytes 1179656 | tf_op jit(solution)/shard_map/ppermute | solution.py:27
  161.6 563.8 %reduce-scatter.18.cloned.1.call-start = ((), (), s32[]{:S(2)}) async-start(), calls=%async_computation.9 | async-start | bytes 2949120 | tf_op jit(solution)/shard_map/reduce_scatter | solution.py:303
  167.9 136.5 %copy-start.20 = (pred[512,1024]{1,0:T(8,128)(4,1)}, pred[512,1024]{1,0:T(8,128)(4,1)S(1)}, u32[]{:S(2)}) copy-start(pred[512,1024]{1,0:T(8,128)(4,1)S(1)} %get-tuple-element.356) | copy-start | bytes 1572868
  240.5 152.2 %copy-start.103 = (f32[384]{0:T(512)}, f32[384]{0:T(512)S(1)}, u32[]{:S(2)}) copy-start(f32[384]{0:T(512)S(1)} %convert_element_type.187) | copy-start | bytes 4612
  336.7 56.0 %copy-start.95 = (f32[3072]{0:T(1024)}, f32[3072]{0:T(1024)S(1)}, u32[]{:S(2)}) copy-start(f32[3072]{0:T(1024)S(1)} %broadcast_multiply_fusion.4) | copy-start | bytes 36868
  339.4 53.3 %copy-start.99 = (f32[3072]{0:T(1024)}, f32[3072]{0:T(1024)S(1)}, u32[]{:S(2)}) copy-start(f32[3072]{0:T(1024)S(1)} %add_rsqrt_fusion) | copy-start | bytes 36868
  473.9 259.4 %reduce-scatter.14.cloned.1.call-start = ((), (), s32[]{:S(2)}) async-start(), calls=%async_computation.7 | async-start | bytes 737280 | tf_op jit(solution)/shard_map/reduce_scatter | solution.py:299
  601.8 53.8 %collective-permute-start.2 = (f32[256,768]{0,1:T(8,128)}, f32[256,768]{0,1:T(8,128)}, u32[]{:S(2)}, u32[]{:S(2)}) collective-permute-start(f32[256,768]{0,1:T(8,128)} %fusion.54), channel_id=1, source_target_pairs={{0,1},{1,2},{2,3},{3,4},{4,5},{5,6},{6,7},{7,8},{8,9},{9,10},{10,1... | collective-permute-start | bytes 2359304 | tf_op jit(solution)/shard_map/ppermute | solution.py:39
  622.5 110.8 %reduce-scatter.16.cloned.1.call-start = ((), (), s32[]{:S(2)}) async-start(), calls=%async_computation.8 | async-start | bytes 2949120 | tf_op jit(solution)/shard_map/reduce_scatter | solution.py:301
  633.2 100.1 %reduce-scatter.12.cloned.1.call-start = ((), (), s32[]{:S(2)}) async-start(), calls=%async_computation.6 | async-start | bytes 2211840 | tf_op jit(solution)/shard_map/reduce_scatter | solution.py:296
  658.1 14.1 %collective-permute-start.3 = (f32[256,768]{0,1:T(8,128)S(1)}, f32[256,768]{0,1:T(8,128)S(1)}, u32[]{:S(2)}, u32[]{:S(2)}) collective-permute-start(f32[256,768]{0,1:T(8,128)S(1)} %get-tuple-element.269), channel_id=1, source_target_pairs={{1,0},{2,1},{3,2},{4,3},{5,4},{6,5},{7,6},{8,7},{9,8},{10,9},{11,1... | collective-permute-start | bytes 2359304 | tf_op jit(solution)/shard_map/ppermute | solution.py:39
  685.4 151.0 %reduce-scatter.20.cloned.1.call-start = ((), (), s32[]{:S(2)}) async-start(), calls=%async_computation.10 | async-start | bytes 663552 | tf_op jit(solution)/shard_map/reduce_scatter | solution.py:310
  772.5 60.7 %collective-permute-start.6 = (f32[16,384]{1,0:T(8,128)S(1)}, f32[16,384]{1,0:T(8,128)S(1)}, u32[]{:S(2)}, u32[]{:S(2)}) collective-permute-start(f32[16,384]{1,0:T(8,128)S(1)} %get-tuple-element.265), channel_id=1, source_target_pairs={{0,1},{1,2},{2,3},{3,4},{4,5},{5,6},{6,7},{8,9},{9,10},{10,11},{11... | collective-permute-start | bytes 73736
  773.8 56.5 %collective-permute-start.7 = (f32[12,384]{1,0:T(8,128)S(1)}, f32[12,384]{1,0:T(8,128)S(1)}, u32[]{:S(2)}, u32[]{:S(2)}) collective-permute-start(f32[12,384]{1,0:T(8,128)S(1)} %slice.582), channel_id=1, source_target_pairs={{0,2},{1,3},{2,4},{3,5},{4,6},{5,7},{8,10},{9,11},{10,12},{11,13},... | collective-permute-start | bytes 55304
  824.1 10.0 %collective-permute-start.4 = (f32[16,1152]{1,0:T(8,128)S(1)}, f32[16,1152]{1,0:T(8,128)S(1)}, u32[]{:S(2)}, u32[]{:S(2)}) collective-permute-start(f32[16,1152]{1,0:T(8,128)S(1)} %get-tuple-element.264), channel_id=1, source_target_pairs={{0,1},{1,2},{2,3},{3,4},{4,5},{5,6},{6,7},{8,9},{9,10},{10,11},{11... | collective-permute-start | bytes 221192
  825.5 9.8 %collective-permute-start.8 = (f32[16,1536]{1,0:T(8,128)S(1)}, f32[16,1536]{1,0:T(8,128)S(1)}, u32[]{:S(2)}, u32[]{:S(2)}) collective-permute-start(f32[16,1536]{1,0:T(8,128)S(1)} %get-tuple-element.266), channel_id=1, source_target_pairs={{0,1},{1,2},{2,3},{3,4},{4,5},{5,6},{6,7},{8,9},{9,10},{10,11},{11... | collective-permute-start | bytes 294920
  828.1 5.9 collective-permute-start.5
  830.2 5.1 collective-permute-start.9
  (166 other events, 1796.0 us)
Sparse Core Ops, SparseCore 0:
  10.9 57.8 all-gather.7
  161.7 51.6 all-gather.5
  474.0 31.6 reduce-scatter.17
  622.6 21.6 reduce-scatter.13
  646.8 32.8 reduce-scatter.15
  685.5 33.2 reduce-scatter.11
  725.6 70.0 reduce-scatter.19
where the time goes:
time: 853 us; the launch traced here: 844 us
  matrix products  276 us (32%)
  blocking collectives  261 us (31%)
  other arithmetic  150 us (18%)
  local copies, waits for them, and re-layouts  104 us (12%)
  starting transfers between devices  25.9 us (3%)
  between operations  20.2 us (2%)
    unnamed x4, blocking collectives  115 us
    unnamed x410, local copies, waits for them, and re-layouts  80.6 us
    all_gather x1, blocking collectives, per_device(): lax.all_gather(params[0], ('dp', 'fsdp'), axis=0, tiled=True)  74.4 us
    all_gather x1, blocking collectives, per_device(): lax.all_gather(params[3], ('dp', 'fsdp'), axis=0, tiled=True)  70.9 us
    convert_element_type x6, other arithmetic, per_device(): (probs * (d_probs - jnp.sum(probs * d_probs, axis=-1, keepdims=True))).as...  61 us
    dot_general x6, matrix products, per_device(): jnp.einsum('qhd,khd->hqk', d_out, values, preferred_element_type=single_p...  46.2 us
    dot_general x6, matrix products, per_device(): jnp.einsum('hqk,khd->qhd', probs_b, values, preferred_element_type=single...  37.4 us
    dot_general x4, matrix products, back_product(): return jnp.dot(left, weight.T, preferred_element_type=jnp.float32)  34.5 us
  transfers between devices with their start and end apart: 17, of which 2 were waited for; matrix products, arithmetic and copies ran while one was open for 50% of the time, Pallas kernels for 0%

commit v1 on v0

v1 whole, which is shorter than its diff:
```python
import functools
import math

import jax
import jax.numpy as jnp
from jax import lax
from jax.experimental import pallas as pl
from jax.experimental.pallas import tpu as pltpu
from jax.sharding import PartitionSpec as P

F32 = jnp.float32
BF16 = jnp.bfloat16
HDIM = 64
EPS = 1e-06
NEG = -1e30
ROOT_HALF = 0.7071067811865476
GAUSS = 0.3989422804014327
LEFT = 112
RIGHT = 160
HALO = LEFT + RIGHT
KEYS = 224
WIN = 256
SHORTEST = 98
AXES = ("dp", "fsdp")
VMEM_BYTES = 63 * 1024 * 1024


def dot(a, b):
    return jnp.dot(a, b, preferred_element_type=F32)


def dot_nt(a, b):
    return lax.dot_general(a, b, (((1,), (1,)), ((), ())), preferred_element_type=F32)


def dot_tn(a, b):
    return lax.dot_general(a, b, (((0,), (0,)), ((), ())), preferred_element_type=F32)


def normed(x):
    centre = x - jnp.mean(x, axis=-1, keepdims=True)
    inverse = lax.rsqrt(jnp.mean(centre * centre, axis=-1, keepdims=True) + EPS)
    return centre * inverse, inverse


def norm_back(grad, xhat, inverse, gain):
    e = grad * gain
    return inverse * (
        e - jnp.mean(e, axis=-1, keepdims=True) - xhat * jnp.mean(e * xhat, axis=-1, keepdims=True)
    )


def colsum(x):
    return jnp.sum(x, axis=0, keepdims=True)


def qkv_rows(rows, weight, gain, shift, bias, width):
    xhat, _ = normed(rows.astype(F32))
    n1 = (xhat * gain + shift).astype(BF16)
    out = dot(n1, weight) + bias
    return jnp.concatenate([out[:, :width] * (1.0 / math.sqrt(HDIM)), out[:, width:]], axis=1).astype(BF16)


def qkv_kernel(tok, tokh, weight, vec, out, outh):
    width = tok.shape[1]
    gain, shift = vec[4:5, :], vec[5:6, :]
    bias = jnp.concatenate([vec[0:1, :], jnp.zeros((1, width), F32), vec[1:2, :]], axis=1)
    out[...] = qkv_rows(tok[...], weight[...], gain, shift, bias, width)

    @pl.when(pl.program_id(0) == pl.num_programs(0) - 1)
    def _():
        outh[...] = qkv_rows(tokh[...], weight[...], gain, shift, bias, width)


def project(tok, tokh, weight, vec):
    rows, width = tok.shape
    tile = 512
    whole = lambda a: pl.BlockSpec(a.shape, lambda i: (0, 0))
    wide = weight.shape[1]
    return pl.pallas_call(
        qkv_kernel,
        grid=(rows // tile,),
        out_shape=(jax.ShapeDtypeStruct((rows, wide), BF16), jax.ShapeDtypeStruct((HALO, wide), BF16)),
        in_specs=[pl.BlockSpec((tile, width), lambda i: (i, 0))] + [whole(a) for a in (tokh, weight, vec)],
        out_specs=(pl.BlockSpec((tile, wide), lambda i: (i, 0)), pl.BlockSpec((HALO, wide), lambda i: (0, 0))),
        name="project",
    )(tok, tokh, weight, vec)


def image_bounds(i, starts, ends):
    s, e = starts[i], ends[i]
    a = pl.multiple_of((s // 16) * 16, 16)
    return s, e, a


def put(ref, a, columns, value, first_row):
    rows = value.shape[0]
    old = ref[pl.ds(a, 16), columns].astype(F32)
    new = value[:16].astype(F32)
    row = lax.broadcasted_iota(jnp.int32, new.shape, 0) + a
    ref[pl.ds(a, 16), columns] = jnp.where(row >= first_row, new, old).astype(ref.dtype)
    ref[pl.ds(a + 16, rows - 16), columns] = value[16:].astype(ref.dtype)


def lane_masks(rows):
    lane = lax.broadcasted_iota(jnp.int32, (rows, 128), 1)
    low = jnp.where(lane < HDIM, 1.0, 0.0)
    return low.astype(BF16), (1.0 - low).astype(BF16)


def attention_forward(i, starts, ends, qkv, probs, att, width):
    s, e, a = image_bounds(i, starts, ends)
    row = lax.broadcasted_iota(jnp.int32, (KEYS, 1), 0) + a
    inside = (row >= s) & (row < e)
    key_bias = jnp.where(inside, 0.0, NEG)
    col = lax.broadcasted_iota(jnp.int32, (1, WIN), 1) + a
    query_on = jnp.where((col >= s) & (col < e), 1.0, 0.0)
    masks = lane_masks(KEYS)
    for pair in range(width // 128):
        lanes = slice(128 * pair, 128 * pair + 128)
        q = qkv[pl.ds(a, WIN), lanes]
        k = qkv[pl.ds(a, KEYS), width + 128 * pair : width + 128 * pair + 128]
        v = qkv[pl.ds(a, KEYS), 2 * width + 128 * pair : 2 * width + 128 * pair + 128]
        total = None
        for half in range(2):
            head = 2 * pair + half
            scores = dot_nt(k * masks[half], q) + key_bias
            top = jnp.max(scores, axis=0, keepdims=True)
            ex = jnp.exp(scores - top)
            p = (ex * (query_on / jnp.sum(ex, axis=0, keepdims=True))).astype(BF16)
            put(probs, a, slice(WIN * head, WIN * head + WIN), p, s)
            part = dot_tn(p, v * masks[half])
            total = part if total is None else total + part
        put(att, a, lanes, total, s)


def attention_backward(i, starts, ends, qkv, probs, att, datt, dqkv, gvec, width, rows):
    s, e, a = image_bounds(i, starts, ends)
    scale = 1.0 / math.sqrt(HDIM)
    row = lax.broadcasted_iota(jnp.int32, (KEYS, 128), 0) + a
    inside = jnp.where((row >= s) & (row < e), 1.0, 0.0).astype(BF16)
    key_masks = [m * inside for m in lane_masks(KEYS)]
    masks = lane_masks(KEYS)
    wide_masks = lane_masks(WIN)
    query = lax.broadcasted_iota(jnp.int32, (WIN, 128), 0) + a
    own = jnp.where((query >= LEFT) & (query < LEFT + rows), 1.0, 0.0)
    group = lax.broadcasted_iota(jnp.int32, (8, width), 1) // HDIM
    heads = jnp.where(group == lax.broadcasted_iota(jnp.int32, (8, width), 0), 1.0, 0.0).astype(BF16)
    both = att[pl.ds(a, WIN), :].astype(F32) * datt[pl.ds(a, WIN), :].astype(F32)
    high = both.astype(BF16)
    delta = dot_nt(heads, high) + dot_nt(heads, (both - high.astype(F32)).astype(BF16))
    for pair in range(width // 128):
        lanes = slice(128 * pair, 128 * pair + 128)
        klanes = slice(width + 128 * pair, width + 128 * pair + 128)
        vlanes = slice(2 * width + 128 * pair, 2 * width + 128 * pair + 128)
        q = qkv[pl.ds(a, WIN), lanes]
        k = qkv[pl.ds(a, KEYS), klanes]
        v = qkv[pl.ds(a, KEYS), vlanes]
        do = datt[pl.ds(a, WIN), lanes]
        dq = dk = dv = None
        for half in range(2):
            head = 2 * pair + half
            p = probs[pl.ds(a, KEYS), WIN * head : WIN * head + WIN]
            dp = dot_nt(v * masks[half], do)
            ds = (p.astype(F32) * (dp - delta[head : head + 1])).astype(BF16)
            dv_part = dot(p, do * wide_masks[half])
            dk_part = dot(ds, q * wide_masks[half])
            dq_part = dot_tn(ds, k * key_masks[half])
            dv = dv_part if dv is None else dv + dv_part
            dk = dk_part if dk is None else dk + dk_part
            dq = dq_part if dq is None else dq + dq_part
        gvec[0:1, lanes] += colsum(dq * own) * scale
        put(dqkv, a, lanes, dq * scale, s)
        put(dqkv, a, klanes, dk, s)
        put(dqkv, a, vlanes, dv, s)


def middle_kernel(
    packs, start_in, end_in, qkv_in, qkvh_in, tok_in, tokh, cot_in, coth, wo, wu, wd, vec, upb,
    out_hbm, dhid_hbm, dqkv_hbm, gvec, gupb, *refs,
):
    if packs:
        packed_hbm, packed, *refs = refs
    gwo, gwu, gwd, qkv, dqkv, probs, att, datt, tok, cot, out_buf, dhid_buf, starts, ends, sems = refs
    rows, width = tok_in.shape
    ff = wu.shape[1]
    extent = rows + HALO
    tile = out_buf.shape[1]
    chunk = 512
    copies = [
        pltpu.make_async_copy(qkvh_in.at[pl.ds(0, LEFT)], qkv.at[pl.ds(0, LEFT)], sems.at[0]),
        pltpu.make_async_copy(qkv_in, qkv.at[pl.ds(LEFT, rows)], sems.at[1]),
        pltpu.make_async_copy(qkvh_in.at[pl.ds(LEFT, RIGHT)], qkv.at[pl.ds(LEFT + rows, RIGHT)], sems.at[2]),
    ]
    later = [
        pltpu.make_async_copy(tok_in, tok, sems.at[3]),
        pltpu.make_async_copy(cot_in, cot, sems.at[4]),
    ]
    for c in copies + later:
        c.start()

    shift = LEFT - lax.axis_index(AXES) * rows
    starts[0] = start_in[0] + shift
    ends[0] = end_in[0] + shift

    def walk(i, n):
        here = ends[i - 1]
        more = here < LEFT + rows
        at = jnp.minimum(here - LEFT, rows - 1)
        starts[i] = here
        ends[i] = end_in[at] + shift
        return jnp.where(more, i + 1, n)

    count = lax.fori_loop(1, starts.shape[0], walk, 1)

    spare = qkv.shape[0] - extent
    qkv[pl.ds(extent, spare), :] = jnp.zeros((spare, qkv.shape[1]), BF16)
    datt[pl.ds(extent, spare), :] = jnp.zeros((spare, width), BF16)
    probs[pl.ds(0, LEFT), :] = jnp.zeros((LEFT, probs.shape[1]), BF16)
    att[pl.ds(0, LEFT), :] = jnp.zeros((LEFT, width), BF16)
    att[pl.ds(LEFT + rows, RIGHT + spare), :] = jnp.zeros((RIGHT + spare, width), BF16)
    dqkv[pl.ds(0, LEFT), :] = jnp.zeros((LEFT, dqkv.shape[1]), BF16)
    for c in copies:
        c.wait()

    @pl.loop(0, count)
    def _(i):
        attention_forward(i, starts, ends, qkv, probs, att, width)

    bo, bd, g2, b2 = (vec[j : j + 1, :] for j in (2, 3, 6, 7))

    def feed(x, c, at, own, sums):
        hid = x.astype(F32) + dot(at, wo[...]) + bo
        xhat, inverse = normed(hid)
        n2 = (xhat * g2 + b2).astype(BF16)
        down = dn2 = None
        if own:
            ct, nt = c.T, n2.T
        for f in range(0, ff, chunk):
            cols = slice(f, f + chunk)
            pre = dot(n2, wu[:, cols]) + upb[0:1, cols]
            half = 0.5 * (1.0 + lax.erf(pre * ROOT_HALF))
            slope = half + pre * jnp.exp(-0.5 * pre * pre) * GAUSS
            dpre = dot_nt(c, wd[cols, :]) * slope
            dpre_b = dpre.astype(BF16)
            part = dot_nt(dpre_b, wu[:, cols])
            dn2 = part if dn2 is None else dn2 + part
            if own:
                act = (pre * half).astype(BF16)
                part = dot(act, wd[cols, :])
                down = part if down is None else down + part
                gwd[:, cols] += dot(ct, act)
                gwu[:, cols] += dot(nt, dpre_b)
                gupb[0:1, cols] += colsum(dpre)
        dhid = c.astype(F32) + norm_back(dn2, xhat, inverse, g2)
        dhid_b = dhid.astype(BF16)
        da = dot_nt(dhid_b, wo[...]).astype(BF16)
        if own:
            gwo[...] += dot_tn(at, dhid_b)
            for j, x in ((2, dhid), (3, c.astype(F32)), (6, dn2 * xhat), (7, dn2)):
                gvec[j : j + 1, :] += colsum(x)
            return hid + down + bd, dhid, da
        return da

    gwo[...] = jnp.zeros_like(gwo)
    gwu[...] = jnp.zeros_like(gwu)
    gwd[...] = jnp.zeros_like(gwd)
    gvec[...] = jnp.zeros_like(gvec)
    gupb[...] = jnp.zeros_like(gupb)
    for c in later:
        c.wait()

    def writes(i, slot):
        at = pl.ds(pl.multiple_of(i * tile, tile), tile)
        return (
            pltpu.make_async_copy(out_buf.at[slot], out_hbm.at[at], sems.at[5 + slot]),
            pltpu.make_async_copy(dhid_buf.at[slot], dhid_hbm.at[at], sems.at[7 + slot]),
        )

    @pl.loop(0, rows // tile)
    def _(i):
        slot = i % 2
        at = pl.multiple_of(i * tile, tile)
        here = pl.ds(pl.multiple_of(LEFT + at, 16), tile)
        layer, dhid, da = feed(tok[pl.ds(at, tile), :], cot[pl.ds(at, tile), :], att[here, :], True, None)
        datt[here, :] = da

        @pl.when(i >= 2)
        def _():
            for w in writes(i - 2, slot):
                w.wait()

        out_buf[slot] = layer.astype(BF16)
        dhid_buf[slot] = dhid
        for w in writes(i, slot):
            w.start()

    sides = jnp.concatenate([att[pl.ds(0, LEFT), :], att[pl.ds(LEFT + rows, RIGHT), :]], axis=0)
    da = feed(tokh[...], coth[...], sides, False, None)
    datt[pl.ds(0, LEFT), :] = da[:LEFT]
    datt[pl.ds(LEFT + rows, RIGHT), :] = da[LEFT:]

    if packs:

        @pl.loop(0, packed.shape[0] // 4)
        def _(i):
            pack_second(i, gwo, gwu, packed)

        pack_down(gwd, packed)
        sent = pltpu.make_async_copy(packed, packed_hbm, sems.at[10])
        sent.start()

    @pl.loop(0, count)
    def _(i):
        attention_backward(i, starts, ends, qkv, probs, att, datt, dqkv, gvec, width, rows)

    last = pltpu.make_async_copy(dqkv.at[pl.ds(LEFT, rows)], dqkv_hbm, sems.at[9])
    last.start()
    n = rows // tile
    for i in range(max(n - 2, 0), n):
        for w in writes(i, i % 2):
            w.wait()
    last.wait()
    if packs:
        sent.wait()


def middle(packs, start, end, qkv, qkvh, tok, tokh, cot, coth, wo, wu, wd, vec, upb):
    rows, width = tok.shape
    ff = wu.shape[1]
    padded = rows + HALO + WIN
    tile = 256
    vmem = pl.BlockSpec(memory_space=pltpu.VMEM)
    smem = pl.BlockSpec(memory_space=pltpu.SMEM)
    anyw = pl.BlockSpec(memory_space=pl.ANY)
    most = rows // SHORTEST + 4
    n = lax.axis_size(AXES)
    S = jax.ShapeDtypeStruct
    sums = [((width, width), F32), ((width, ff), F32), ((width, ff), F32)]
    slabs = (n, 16, SECOND)
    return pl.pallas_call(
        functools.partial(middle_kernel, packs),
        out_shape=[
            S((rows, width), BF16), S((rows, width), F32), S((rows, 3 * width), BF16), S((8, width), F32), S((8, ff), F32),
        ] + ([S(slabs, BF16)] if packs else [S(*a) for a in sums]),
        in_specs=[smem, smem, anyw, anyw, anyw, vmem, anyw, vmem, vmem, vmem, vmem, vmem, vmem],
        out_specs=[anyw, anyw, anyw, vmem, vmem] + ([anyw] if packs else [vmem] * 3),
        scratch_shapes=([pltpu.VMEM(slabs, BF16)] + [pltpu.VMEM(*a) for a in sums] if packs else [])
        + [
            pltpu.VMEM((padded, 3 * width), BF16),
            pltpu.VMEM((padded, 3 * width), BF16),
            pltpu.VMEM((padded, width // HDIM * WIN), BF16),
            pltpu.VMEM((padded, width), BF16),
            pltpu.VMEM((padded, width), BF16),
            pltpu.VMEM((rows, width), BF16),
            pltpu.VMEM((rows, width), BF16),
            pltpu.VMEM((2, tile, width), BF16),
            pltpu.VMEM((2, tile, width), F32),
            pltpu.SMEM((most,), jnp.int32),
            pltpu.SMEM((most,), jnp.int32),
            pltpu.SemaphoreType.DMA((11,)),
        ],
        compiler_params=pltpu.CompilerParams(vmem_limit_bytes=VMEM_BYTES),
        name="middle",
    )(start, end, qkv, qkvh, tok, tokh, cot, coth, wo, wu, wd, vec, upb)


def last_kernel(packs, tok, dhid, dqkv, weight, vec, gvec, gupb, dx, *refs):
    packed, gw, sums = refs if packs else (None,) + refs
    width = tok.shape[1]

    @pl.when(pl.program_id(0) == 0)
    def _():
        gw[...] = jnp.zeros_like(gw)
        sums[...] = gvec[...]

    gain, shift = vec[4:5, :], vec[5:6, :]
    xhat, inverse = normed(tok[...].astype(F32))
    n1 = (xhat * gain + shift).astype(BF16)
    d = dqkv[...]
    gw[...] += dot_tn(n1, d)
    dn1 = dot_nt(d, weight[...])
    sums[1:2, :] += colsum(d[:, 2 * width :].astype(F32))
    sums[4:5, :] += colsum(dn1 * xhat)
    sums[5:6, :] += colsum(dn1)
    dx[...] = dhid[...] + norm_back(dn1, xhat, inverse, gain)

    if packs:

        @pl.when(pl.program_id(0) == pl.num_programs(0) - 1)
        def _():
            @pl.loop(0, packed.shape[0] // 4)
            def _(i):
                pack_first(i, gw, packed)

            pack_small(sums[...], gupb[...], packed)


def last(packs, tok, dhid, dqkv, weight, vec, gvec, gupb):
    rows, width = tok.shape
    wide = weight.shape[1]
    tile = 512
    n = lax.axis_size(AXES)
    whole = lambda a: pl.BlockSpec(a, lambda i: (0,) * len(a))
    rowed = lambda n: pl.BlockSpec((tile, n), lambda i: (i, 0))
    S = jax.ShapeDtypeStruct
    sums = [(width, wide), (8, width)]
    return pl.pallas_call(
        functools.partial(last_kernel, packs),
        grid=(rows // tile,),
        out_shape=[S((rows, width), F32)] + ([S((n, 16, FIRST), BF16)] if packs else [S(a, F32) for a in sums]),
        in_specs=[rowed(width), rowed(width), rowed(wide)] + [whole(a.shape) for a in (weight, vec, gvec, gupb)],
        out_specs=[rowed(width)] + ([whole((n, 16, FIRST))] if packs else [whole(a) for a in sums]),
        scratch_shapes=[pltpu.VMEM(a, F32) for a in sums] if packs else [],
        compiler_params=pltpu.CompilerParams(vmem_limit_bytes=VMEM_BYTES),
        name="last",
    )(tok, dhid, dqkv, weight, vec, gvec, gupb)


COLS, ROWS_UP, LAYERS, CORES = 2, 2, 4, 2
LANES = 3584
SMALL, QKV, OUT, UP, DOWN = 0, 128, 1280, 1664, 2432
PIECES = ((0, 640, 0), (640, 1280, 1), (1280, 2432, 0), (2432, 3584, 1))
MESH = pl.DeviceIdType.MESH


def here():
    dp, fs = lax.axis_index("dp"), lax.axis_index("fsdp")
    return dp // CORES, dp % CORES, fs // ROWS_UP, fs % ROWS_UP


def place(x, c, z, y):
    return (x * CORES + c, z * ROWS_UP + y)


def number(x, c, z, y):
    return (x * CORES + c) * (LAYERS * ROWS_UP) + z * ROWS_UP + y


def greet(ids):
    barrier = pltpu.get_barrier_semaphore()
    for d in ids:
        pl.semaphore_signal(barrier, inc=1, device_id=d, device_id_type=MESH)
    pl.semaphore_wait(barrier, len(ids))


def remote(src, dst, send, recv, to):
    return pltpu.make_async_remote_copy(src_ref=src, dst_ref=dst, send_sem=send, recv_sem=recv, device_id=to, device_id_type=MESH)


def along(step):
    dp, fs = lax.axis_size("dp"), lax.axis_size("fsdp")
    at = lax.rem(lax.axis_index("dp") * fs + lax.axis_index("fsdp") + step + dp * fs, dp * fs)
    return (at // fs, lax.rem(at, fs))


class Gather:
    def __init__(self, slabs, send, recv):
        self.slabs, self.send, self.recv = slabs, send, recv
        self.x, self.c, self.z, self.y = here()

    def copy(self, piece, slab, to):
        lo, hi, _ = PIECES[piece]
        ref = self.slabs.at[slab, :, lo:hi]
        return remote(ref, ref, self.send.at[piece], self.recv.at[piece, slab], to)

    def give(self, piece, slab, axes):
        x, c, z, y = self.x, self.c, self.z, self.y
        for axis in axes:
            if axis == "z":
                for d in range(1, LAYERS):
                    self.copy(piece, slab, place(x, c, lax.rem(z + d, LAYERS), y)).start()
            else:
                to = {"x": place(1 - x, c, z, y), "y": place(x, c, z, 1 - y), "c": place(x, 1 - c, z, y)}[axis]
                self.copy(piece, slab, to).start()

    def own(self, piece):
        self.give(piece, number(self.x, self.c, self.z, self.y), "zxyc")

    def take(self, piece, slab):
        self.copy(piece, slab, place(self.x, self.c, self.z, self.y)).wait_recv()

    def stage(self, piece, level):
        x, c, z, y = self.x, self.c, self.z, self.y
        order = PIECES[piece][2]
        second, third = ("x", "y") if order == 0 else ("y", "x")
        if level == 0:
            group = [(x, lax.rem(z + d, LAYERS), y) for d in range(1, LAYERS)]
            passed = second + third + "c"
        elif level == 1:
            group = [(1 - x, lax.rem(z + d, LAYERS), y) if order == 0 else (x, lax.rem(z + d, LAYERS), 1 - y) for d in range(LAYERS)]
            passed = third + "c"
        else:
            if order == 0:
                group = [(x if s == 0 else 1 - x, lax.rem(z + d, LAYERS), 1 - y) for s in range(2) for d in range(LAYERS)]
            else:
                group = [(1 - x, lax.rem(z + d, LAYERS), y if s == 0 else 1 - y) for s in range(2) for d in range(LAYERS)]
            passed = "c"
        for gx, gz, gy in group:
            slab = number(gx, c, gz, gy)
            self.take(piece, slab)
            self.give(piece, slab, passed)

    def siblings(self, piece):
        x, c, z, y = self.x, self.c, self.z, self.y
        for dx in range(COLS):
            for dy in range(ROWS_UP):
                for d in range(LAYERS):
                    self.take(piece, number(x if dx == 0 else 1 - x, 1 - c, lax.rem(z + d, LAYERS), y if dy == 0 else 1 - y))

    def finish(self, piece):
        lo, hi, _ = PIECES[piece]
        ref = self.slabs.at[pl.ds(0, 31), :, lo:hi]
        remote(ref, ref, self.send.at[piece], self.recv.at[piece, 0], place(self.x, self.c, self.z, self.y)).wait_send()


def gather_kernel(
    small, wqkv_in, wo_in, wu_in, wd_in, tok, cot,
    wqkv, wo, wu, wd, vec, upb, tokh, coth,
    slabs, send, recv, side_send, side_recv,
):
    x, c, z, y = here()
    me = number(x, c, z, y)
    rows, width = tok.shape
    n = slabs.shape[0]
    own = slabs.at[me]
    own[:, SMALL:QKV] = small[...]
    split = 768
    up = wu_in[...].astype(F32)
    top = jnp.concatenate([wqkv_in[...].astype(F32), wo_in[...].astype(F32), up[:, :split]], axis=1)
    rest = jnp.concatenate([up[4 * i : 4 * i + 4, split:] for i in range(3)], axis=1)
    own[:, QKV:DOWN] = jnp.concatenate([top, rest], axis=0).astype(BF16)
    for i in range(3):
        own[:, DOWN + width * i : DOWN + width * (i + 1)] = wd_in[16 * i : 16 * i + 16, :]

    greet(
        [place(x, c, lax.rem(z + d, LAYERS), y) for d in range(1, LAYERS)]
        + [place(1 - x, c, z, y), place(x, c, z, 1 - y), place(x, 1 - c, z, y), along(1), along(-1)]
    )
    g = Gather(slabs, send, recv)
    for p in (0, 1):
        g.own(p)
    sides = []
    for j, (src, dst) in enumerate(((tok, tokh), (cot, coth))):
        sides.append(remote(src.at[pl.ds(rows - LEFT, LEFT)], dst.at[pl.ds(0, LEFT)], side_send.at[2 * j], side_recv.at[2 * j], along(1)))
        sides.append(remote(src.at[pl.ds(0, RIGHT)], dst.at[pl.ds(LEFT, RIGHT)], side_send.at[2 * j + 1], side_recv.at[2 * j + 1], along(-1)))
    for p in (0, 1):
        g.stage(p, 0)
    for p in (2, 3):
        g.own(p)
    for s in sides:
        s.start()
    for level in (1, 2):
        for p in (0, 1):
            g.stage(p, level)
    for level in (0, 1, 2):
        for p in (2, 3):
            g.stage(p, level)
    for p in range(4):
        g.siblings(p)
    for s in sides:
        s.wait()
    for p in range(4):
        g.finish(p)

    @pl.loop(0, n // 4)
    def _(i):
        at = pl.ds(pl.multiple_of(48 * i, 16), 48)
        parts = [slabs[4 * i + d, :, QKV:DOWN].astype(F32) for d in range(4)]
        full = jnp.concatenate([p[:12] for p in parts], axis=0).astype(BF16)
        wqkv[at, :] = full[:, : OUT - QKV]
        wo[at, :] = full[:, OUT - QKV : UP - QKV]
        wu[at, :split] = full[:, UP - QKV :]
        wu[at, split:] = jnp.concatenate([p[12:, split * j : split * (j + 1)] for p in parts for j in range(3)], axis=0).astype(BF16)
        for d in range(4):
            for j in range(3):
                wd[pl.ds(pl.multiple_of(48 * (4 * i + d) + 16 * j, 16), 16), :] = slabs[4 * i + d, :, DOWN + width * j : DOWN + width * (j + 1)]

    lane = lax.broadcasted_iota(jnp.int32, (8, 128), 1)
    lines = [jnp.zeros((8, 128), F32) for _ in range(width // 128)]
    ups = [jnp.zeros((8, 128), F32) for _ in range(upb.shape[1] // 128)]
    for k in range(n):
        s = slabs[k, :, SMALL:QKV].astype(F32)
        for tiles, block, size in ((lines, s[:8], 12), (ups, s[8:], 48)):
            t, by = divmod(size * k, 128)
            moved = pltpu.roll(block, by, 1) if by else block
            if by + size <= 128:
                tiles[t] = tiles[t] + moved
            else:
                tiles[t] = tiles[t] + jnp.where(lane >= by, moved, 0.0)
                tiles[t + 1] = tiles[t + 1] + jnp.where(lane < by, moved, 0.0)
    vec[...] = jnp.concatenate(lines, axis=1)
    upb[...] = jnp.concatenate(ups, axis=1)


def gather_all(small, wqkv, wo, wu, wd, tok, cot):
    n = lax.axis_size(AXES)
    rows, width = tok.shape
    vmem = pl.BlockSpec(memory_space=pltpu.VMEM)
    anyw = pl.BlockSpec(memory_space=pl.ANY)
    S = jax.ShapeDtypeStruct
    return pl.pallas_call(
        gather_kernel,
        out_shape=(
            S((width, wqkv.shape[1]), BF16), S((width, width), BF16), S((width, wu.shape[1]), BF16), S((wd.shape[0] * n, width), BF16),
            S((8, width), F32), S((8, wu.shape[1]), F32), S((HALO, width), BF16), S((HALO, width), BF16),
        ),
        in_specs=[vmem] * 5 + [anyw] * 2,
        out_specs=(vmem,) * 6 + (anyw,) * 2,
        scratch_shapes=[
            pltpu.VMEM((n, 16, LANES), BF16),
            pltpu.SemaphoreType.DMA((4,)),
            pltpu.SemaphoreType.DMA((4, n)),
            pltpu.SemaphoreType.DMA((4,)),
            pltpu.SemaphoreType.DMA((4,)),
        ],
        compiler_params=pltpu.CompilerParams(collective_id=0, has_side_effects=True, vmem_limit_bytes=VMEM_BYTES),
        name="gather",
    )(small, wqkv, wo, wu, wd, tok, cot)


FIRST, SECOND = 1024, 2688
SPARE_QKV, SPARE_UP = 896, 1152
DOWN_AT = 1536
SHARES = ((1, 0, 1408, 0), (1, 1408, 2688, 1), (0, 0, 512, 0), (0, 512, 1024, 1))


def pack_first(i, gw, out):
    x = gw[pl.ds(pl.multiple_of(48 * i, 16), 48), :]
    for d in range(4):
        part = x[12 * d : 12 * d + 12]
        rest = jnp.concatenate([part[4 * j : 4 * j + 4, SPARE_QKV:] for j in range(3)] + [jnp.zeros((4, 128), F32)], axis=1)
        out[4 * i + d, :, 128:] = jnp.concatenate([part[:, :SPARE_QKV], rest], axis=0).astype(BF16)


def pack_second(i, gwo, gwu, out):
    at = pl.ds(pl.multiple_of(48 * i, 16), 48)
    x = jnp.concatenate([gwo[at, :], gwu[at, :]], axis=1)
    width = gwo.shape[1]
    for d in range(4):
        part = x[12 * d : 12 * d + 12]
        rest = jnp.concatenate([part[4 * j : 4 * j + 4, DOWN_AT:] for j in range(3)] + [jnp.zeros((4, width), F32)], axis=1)
        out[4 * i + d, :, :DOWN_AT] = jnp.concatenate([part[:, :DOWN_AT], rest], axis=0).astype(BF16)


def pack_down(gwd, out):
    width, ff = gwd.shape
    for b in range(ff // 128):
        turned = gwd[:, 128 * b : 128 * b + 128].T.astype(BF16)
        for r in range(8):
            k, i = divmod(8 * b + r, 3)
            out[k, :, DOWN_AT + width * i : DOWN_AT + width * (i + 1)] = turned[16 * r : 16 * r + 16]


def pack_small(vectors, wide, out):
    lane = lax.broadcasted_iota(jnp.int32, (8, 128), 1)
    for k in range(out.shape[0]):
        blocks = []
        for src, size in ((vectors, 12), (wide, 48)):
            t, by = divmod(size * k, 128)
            block = src[:, 128 * t : 128 * t + 128]
            if by:
                block = pltpu.roll(block, 128 - by, 1)
                if by + size > 128:
                    block = jnp.where(lane < 128 - by, block, pltpu.roll(src[:, 128 * t + 128 : 128 * t + 256], 128 - by, 1))
            blocks.append(block)
        out[k, :, 0:128] = jnp.concatenate(blocks, axis=0).astype(BF16)


class Scatter:
    def __init__(self, share, parts, mine, others, first, second, third, sems):
        self.block, self.lo, self.hi, self.order = SHARES[share]
        self.share, self.parts = share, parts[self.block]
        self.sum, self.core, self.first, self.second, self.third = mine, others, first, second, third
        self.send, self.core_sem, self.first_sem, self.second_sem, self.third_sem = sems
        self.x, self.c, self.z, self.y = here()
        self.lanes = slice(self.lo, self.hi)
        self.wide = slice(0, self.hi - self.lo)

    def part(self, da, db, d, core):
        dx, dy = (db, da) if self.order == 0 else (da, db)
        slab = number(1 - self.x if dx else self.x, core, lax.rem(self.z + d, LAYERS), 1 - self.y if dy else self.y)
        return self.parts.at[slab, :, self.lanes]

    def move(self, src, dst, sem, to):
        return remote(src, dst, self.send.at[self.share], sem, to)

    def slot(self, da, db, d):
        return (da * 2 + db) * LAYERS + d

    def to_core(self, da, db, d):
        s = self.slot(da, db, d)
        to = place(self.x, 1 - self.c, self.z, self.y)
        return self.move(self.part(da, db, d, 1 - self.c), self.core.at[self.share, s, :, self.wide], self.core_sem.at[self.share, s], to)

    def to_first(self, db, d):
        s = self.slot(1, db, d)
        to = place(self.x, self.c, self.z, 1 - self.y) if self.order == 0 else place(1 - self.x, self.c, self.z, self.y)
        at = db * LAYERS + d
        return self.move(self.sum.at[self.share, s, :, self.wide], self.first.at[self.share, at, :, self.wide], self.first_sem.at[self.share, at], to)

    def to_second(self, d):
        s = self.slot(0, 1, d)
        to = place(1 - self.x, self.c, self.z, self.y) if self.order == 0 else place(self.x, self.c, self.z, 1 - self.y)
        return self.move(self.sum.at[self.share, s, :, self.wide], self.second.at[self.share, d, :, self.wide], self.second_sem.at[self.share, d], to)

    def to_third(self, d):
        s = self.slot(0, 0, d)
        to = place(self.x, self.c, lax.rem(self.z + d, LAYERS), self.y)
        return self.move(self.sum.at[self.share, s, :, self.wide], self.third.at[self.share, d - 1, :, self.wide], self.third_sem.at[self.share, d - 1], to)

    def begin(self):
        for da, db in ((1, 1), (1, 0), (0, 1), (0, 0)):
            for d in (1, 2, 3, 0):
                self.to_core(da, db, d).start()

    def total(self, da, db, d):
        s = self.slot(da, db, d)
        self.to_core(da, db, d).wait_recv()
        t = self.part(da, db, d, self.c)[...].astype(F32) + self.core[self.share, s, :, self.wide].astype(F32)
        if da == 0:
            self.to_first(db, d).wait_recv()
            t = t + self.first[self.share, db * LAYERS + d, :, self.wide].astype(F32)
            if db == 0:
                self.to_second(d).wait_recv()
                t = t + self.second[self.share, d, :, self.wide].astype(F32)
        return t

    def level(self, n):
        for da, db, d in {
            0: [(1, db, d) for db in (1, 0) for d in (1, 2, 3, 0)],
            1: [(0, 1, d) for d in (1, 2, 3, 0)],
            2: [(0, 0, d) for d in (1, 2, 3)],
        }[n]:
            self.sum[self.share, self.slot(da, db, d), :, self.wide] = self.total(da, db, d).astype(BF16)
            (self.to_first(db, d) if n == 0 else self.to_second(d) if n == 1 else self.to_third(d)).start()

    def result(self):
        t = self.total(0, 0, 0)
        for d in (1, 2, 3):
            self.to_third(d).wait_recv()
            t = t + self.third[self.share, d - 1, :, self.wide].astype(F32)
        return t

    def finish(self):
        ref = self.parts.at[pl.ds(0, 31), :, self.lanes]
        self.move(ref, ref, self.core_sem.at[self.share, 0], place(self.x, self.c, self.z, self.y)).wait_send()


def scatter_kernel(first_in, second_in, gqkv, gwo, gwu, gwd, small, mine, core, first, second, third, *sems):
    x, c, z, y = here()
    greet(
        [place(x, c, lax.rem(z + d, LAYERS), y) for d in range(1, LAYERS)]
        + [place(1 - x, c, z, y), place(x, c, z, 1 - y), place(x, 1 - c, z, y)]
    )
    shares = [Scatter(i, (first_in, second_in), mine, core, first, second, third, sems) for i in range(len(SHARES))]
    for s in shares:
        s.begin()
    for n in range(3):
        for s in shares:
            s.level(n)
    two, one = jnp.concatenate([s.result() for s in shares[:2]], axis=1), jnp.concatenate([s.result() for s in shares[2:]], axis=1)
    width = gwo.shape[1]
    gqkv[:, :SPARE_QKV] = one[:12, 128:]
    gwo[...] = two[:12, :width]
    gwu[:, :SPARE_UP] = two[:12, width:DOWN_AT]
    for j in range(3):
        gqkv[4 * j : 4 * j + 4, SPARE_QKV:] = one[12:, 128 + 256 * j : 128 + 256 * (j + 1)]
        gwu[4 * j : 4 * j + 4, SPARE_UP:] = two[12:, width * j : width * (j + 1)]
        gwd[16 * j : 16 * j + 16, :] = two[:, DOWN_AT + width * j : DOWN_AT + width * (j + 1)]
    small[...] = one[:, :128]
    for s in shares:
        s.finish()


def scatter_all(first, second, width, ff):
    n = first.shape[0]
    vmem = pl.BlockSpec(memory_space=pltpu.VMEM)
    S = jax.ShapeDtypeStruct
    own = width // n
    k = len(SHARES)
    widest = max(hi - lo for _, lo, hi, _ in SHARES)
    return pl.pallas_call(
        scatter_kernel,
        out_shape=(S((own, 3 * width), F32), S((own, width), F32), S((own, ff), F32), S((ff // n, width), F32), S((16, 128), F32)),
        in_specs=[vmem, vmem],
        out_specs=(vmem,) * 5,
        scratch_shapes=[
            pltpu.VMEM((k, 16, 16, widest), BF16),
            pltpu.VMEM((k, 16, 16, widest), BF16),
            pltpu.VMEM((k, 8, 16, widest), BF16),
            pltpu.VMEM((k, 4, 16, widest), BF16),
            pltpu.VMEM((k, 3, 16, widest), BF16),
            pltpu.SemaphoreType.DMA((k,)),
            pltpu.SemaphoreType.DMA((k, 16)),
            pltpu.SemaphoreType.DMA((k, 8)),
            pltpu.SemaphoreType.DMA((k, 4)),
            pltpu.SemaphoreType.DMA((k, 3)),
        ],
        compiler_params=pltpu.CompilerParams(collective_id=1, has_side_effects=True, vmem_limit_bytes=VMEM_BYTES),
        name="scatter",
    )(first, second)


def small_parameters(vectors, wide):
    block = jnp.stack(list(vectors), axis=0)
    block = jnp.pad(block, ((0, 0), (0, 128 - block.shape[1])))
    return jnp.concatenate([block, jnp.pad(wide[None, :], ((0, 7), (0, 128 - wide.shape[0])))], axis=0)


def per_device(
    tokens, cotangent, image_start, image_end, qkv_weight, q_bias, v_bias, out_weight, out_bias, up_weight, up_bias,
    down_weight, down_bias, first_gain, first_bias, second_gain, second_bias,
):
    width, ff = tokens.shape[1], up_weight.shape[1]
    vectors = (q_bias, v_bias, out_bias, down_bias, first_gain, first_bias, second_gain, second_bias)
    packs = lax.axis_size("dp") == COLS * CORES and lax.axis_size("fsdp") == LAYERS * ROWS_UP
    if packs:
        small = small_parameters(vectors, up_bias)
        wqkv, wo, wu, wd, vec, upb, tokh, coth = gather_all(small, qkv_weight, out_weight, up_weight, down_weight, tokens, cotangent)
    else:
        whole = lambda a: lax.all_gather(a, AXES, axis=0, tiled=True)
        wqkv, wo, wu, wd = (whole(a) for a in (qkv_weight, out_weight, up_weight, down_weight))
        vec = jnp.stack([whole(a).astype(F32) for a in vectors])
        upb = jnp.broadcast_to(whole(up_bias).astype(F32)[None, :], (8, ff))
        n = lax.axis_size(AXES)
        up, down = [(i, i + 1) for i in range(n - 1)], [(i + 1, i) for i in range(n - 1)]
        side = lambda a: jnp.concatenate([lax.ppermute(a[a.shape[0] - LEFT :], AXES, up), lax.ppermute(a[:RIGHT], AXES, down)])
        tokh, coth = side(tokens), side(cotangent)
    qkv, qkvh = project(tokens, tokh, wqkv, vec)
    layer, dhid, dqkv, gvec, gupb, *grads = middle(
        packs, image_start, image_end, qkv, qkvh, tokens, tokh, cotangent, coth, wo, wu, wd, vec, upb
    )
    dx, *grads1 = last(packs, tokens, dhid, dqkv, wqkv, vec, gvec, gupb)
    if packs:
        gqkv, gwo, gwu, gwd, sums = scatter_all(grads1[0], grads[0], width, ff)
        sums, ups = sums[:8, : q_bias.shape[0]], sums[8, : up_bias.shape[0]]
    else:
        reduced = lambda a: lax.psum_scatter(a, AXES, scatter_dimension=0, tiled=True)
        gqkv, gwo, gwu, gwd = (reduced(a) for a in (grads1[0], grads[0], grads[1], grads[2].T))
        sums, ups = reduced(grads1[1].T).T, reduced(gupb[0])
    return (
        layer, dx, gqkv, sums[0], sums[1], gwo, sums[2], gwu, ups, gwd, sums[3], sums[4], sums[5], sums[6], sums[7],
    )


def solution(mesh):
    both = P(AXES, None)
    one = P(AXES)
    in_specs = (both, both, one, one, both, one, one, both, one, both, one, both, one, one, one, one, one)
    out_specs = (both, both, both, one, one, both, one, both, one, both, one, one, one, one, one)
    return jax.shard_map(per_device, mesh=mesh, in_specs=in_specs, out_specs=out_specs, check_vma=False)
```

time: 853 us -> 216 us (0.25)
  matrix products: 276 us -> 0 us
  blocking collectives: 261 us -> 0 us
  Pallas kernels: 0 us -> 203 us
  other arithmetic: 150 us -> 1.25 us
  local copies, waits for them, and re-layouts: 104 us -> 9.42 us
  starting transfers between devices: 25.9 us -> 0 us
  between operations: 20.2 us -> 0.68 us
    dot_general x48 -> x0, matrix products: 276 us -> none  [the longest x6 46.2 us: per_device(): jnp.einsum('qhd,khd->hqk', d_out, values, preferred_element_type=single_p...]
    pallas_call x0 -> x5, Pallas kernels: none -> 203 us  [the longest x1 102 us: middle(): pl.pallas_call(functools.partial(middle_kernel, packs), out_shape=[S((row...]
    all_gather x2 -> x0, blocking collectives: 145 us -> none  [the longest x1 74.4 us: per_device(): lax.all_gather(params[0], ('dp', 'fsdp'), axis=0, tiled=True)]
    unnamed x4 -> x0, blocking collectives: 115 us -> none
    unnamed x410 -> x4, local copies, waits for them, and re-layouts: 80.6 us -> 5.93 us
    convert_element_type x16 -> x0, other arithmetic: 70.9 us -> none  [the longest x6 61 us: per_device(): (probs * (d_probs - jnp.sum(probs * d_probs, axis=-1, keepdims=True))).as...]
    reduce_sum x14 -> x0, other arithmetic: 45 us -> none  [the longest x6 20.9 us: per_device(): lse = top + jnp.log(jnp.sum(jnp.exp(scores - top), axis=-1, keepdims=True))]
    concatenate x5 -> x1, other arithmetic: 15.7 us -> 1.25 us  [small_parameters(): jnp.concatenate([block, jnp.pad(wide[None, :], ((0, 7), (0, 128 - wide.sh...]
  transfers between devices with their start and end apart: 17 -> 0, of which waited for: 2 -> 0; matrix products, arithmetic and copies ran while one was open for 50% -> 0% of each run, Pallas kernels for 0% -> 0%
where the time goes in v1:
time: 216 us; the launch traced here: 215 us
  Pallas kernels  203 us (94%)
  local copies, waits for them, and re-layouts  9.42 us (4%)
    pallas_call x1, Pallas kernels, middle(): pl.pallas_call(functools.partial(middle_kernel, packs), out_shape=[S((row...  102 us
    pallas_call x1, Pallas kernels, gather_all(): pl.pallas_call(gather_kernel, out_shape=(S((width, wqkv.shape[1]), BF16),...  39.7 us
    pallas_call x1, Pallas kernels, scatter_all(): pl.pallas_call(scatter_kernel, out_shape=(S((own, 3 * width), F32), S((ow...  36.2 us
    pallas_call x1, Pallas kernels, last(): pl.pallas_call(functools.partial(last_kernel, packs), grid=(rows // tile,...  15.3 us
    pallas_call x1, Pallas kernels, project(): pl.pallas_call(qkv_kernel, grid=(rows // tile,), out_shape=(jax.ShapeDtyp...  10.1 us
    unnamed x4, local copies, waits for them, and re-layouts  5.93 us

profile of v1, /device:TPU:0, one launch (start us, length us, event | category | flops | bytes accessed | tf_op | source)
XLA Modules:
  0.0 214.8 jit_solution(8507529286921748478)
XLA Ops:
  0.6 0.8 stack.35
  1.4 1.3 fusion.2.small
  2.7 39.7 %gather.1 = (bf16[384,1152]{1,0:T(8,128)(2,1)}, bf16[384,384]{1,0:T(8,128)(2,1)}, bf16[384,1536]{1,0:T(8,128)(2,1)}, bf16[1536,384]{1,0:T(8,128)(2,1)}, f32[8,38...) custom-call(bf16[16,128]{1,0:T(8,128)(2,1)} %fusion.2.small, ...), custom_call_target="tpu_custom_call" | custom-call | tf_op jit(solution)/shard_map/gather/pallas_call | solution.py:602
  42.4 10.1 %project.1 = (bf16[3072,1152]{1,0:T(8,128)(2,1)}, bf16[272,1152]{1,0:T(8,128)(2,1)}) custom-call(bf16[3072,384]{1,0:T(8,128)(2,1)} %tok.5, bf16[272,384]{1,0:T(8,128)(2,1)} %get-tuple-element.38.tokh, bf16[384,1152]{1,0:T(8,128)(2,1)} %get-tuple-element.39.weight, f32[8,384]{1,0:T(8,128)} %get-tuple-element.40.vec), custom_call_target="tpu_custom_call" | custom-call | tf_op jit(solution)/shard_map/project/pallas_call | solution.py:80
  52.5 102.2 %middle.1 = (bf16[3072,384]{1,0:T(8,128)(2,1)}, f32[3072,384]{1,0:T(8,128)}, bf16[3072,1152]{1,0:T(8,128)(2,1)}, f32[8,384]{1,0:T(8,128)}, f32[8,1536]{1,0:T(8,128)}, /*index=5*/bf16[32,16,2688]{2,1,0:T(8,128)(2,1)}) custom-call(s32[3072]{0:T(1024)} %start_in.1, s32[3072]{0:T(1024)} %end_in.1, bf16[3072,1152]{1,0:T(8,128)(2,1)} %get-tuple-element.41.qkv_in, ...), custom_call_target="tpu_custom_call" | custom-call | tf_op jit(solution)/shard_map/middle/pallas_call | solution.py:341
  154.7 15.3 %last.1 = (f32[3072,384]{1,0:T(8,128)}, bf16[32,16,1024]{2,1,0:T(8,128)(2,1)}) custom-call(bf16[3072,384]{1,0:T(8,128)(2,1)} %tok.5, f32[3072,384]{1,0:T(8,128)} %get-tuple-element.49.dhid, bf16[3072,1152]{1,0:T(8,128)(2,1)} %get-tuple-element.50.dqkv, bf16[384,1152]{1,0:T(8,128)(2,1)} %get-tuple-element.39.weight, f32[8,384]{1,0:T(8,128)} %get-tuple-element.40.vec, ...), custom_call_target="tpu_custom_call" | custom-call | tf_op jit(solution)/shard_map/last/pallas_call | solution.py:408
  169.9 36.2 %scatter.1 = (f32[12,1152]{1,0:T(8,128)}, f32[12,384]{1,0:T(8,128)}, f32[12,1536]{1,0:T(8,128)}, f32[48,384]{1,0:T(8,128)}, f32[16,128]{1,0:T(8,128)}) custom-call(bf16[32,16,1024]{2,1,0:T(8,128)(2,1)} %get-tuple-element.54.first_in, bf16[32,16,2688]{2,1,0:T(8,128)(2,1)} %get-tuple-element.55.second_in), custom_call_target="tpu_custom_call" | custom-call | tf_op jit(solution)/shard_map/scatter/pallas_call | solution.py:783
  206.2 1.2 slice_bitcast_fusion.5
  207.3 1.5 slice_bitcast_fusion
  208.9 1.5 copy.36
  210.4 1.3 copy.37
  211.7 1.5 copy.38
  213.3 1.5 copy.39

commit v2 on v1

--- a/solution.py
+++ b/solution.py
@@ -20,7 +20,8 @@
 HALO = LEFT + RIGHT
 KEYS = 224
 WIN = 256
-SHORTEST = 98
+SPARE = 64
+SHORTEST, LONGEST = 98, 197
 AXES = ("dp", "fsdp")
 VMEM_BYTES = 63 * 1024 * 1024
 
@@ -93,12 +94,10 @@
     return s, e, a
 
 
-def put(ref, a, columns, value, first_row):
+def put(ref, a, columns, value, first_row, old):
     rows = value.shape[0]
-    old = ref[pl.ds(a, 16), columns].astype(F32)
-    new = value[:16].astype(F32)
-    row = lax.broadcasted_iota(jnp.int32, new.shape, 0) + a
-    ref[pl.ds(a, 16), columns] = jnp.where(row >= first_row, new, old).astype(ref.dtype)
+    row = lax.broadcasted_iota(jnp.int32, (16, value.shape[1]), 0) + a
+    ref[pl.ds(a, 16), columns] = jnp.where(row >= first_row, value[:16].astype(F32), old[:, columns].astype(F32)).astype(ref.dtype)
     ref[pl.ds(a + 16, rows - 16), columns] = value[16:].astype(ref.dtype)
 
 
@@ -116,6 +115,7 @@
     col = lax.broadcasted_iota(jnp.int32, (1, WIN), 1) + a
     query_on = jnp.where((col >= s) & (col < e), 1.0, 0.0)
     masks = lane_masks(KEYS)
+    old_probs, old_att = probs[pl.ds(a, 16), :], att[pl.ds(a, 16), :]
     for pair in range(width // 128):
         lanes = slice(128 * pair, 128 * pair + 128)
         q = qkv[pl.ds(a, WIN), lanes]
@@ -128,10 +128,10 @@
             top = jnp.max(scores, axis=0, keepdims=True)
             ex = jnp.exp(scores - top)
             p = (ex * (query_on / jnp.sum(ex, axis=0, keepdims=True))).astype(BF16)
-            put(probs, a, slice(WIN * head, WIN * head + WIN), p, s)
+            put(probs, a, slice(WIN * head, WIN * head + WIN), p, s, old_probs)
             part = dot_tn(p, v * masks[half])
             total = part if total is None else total + part
-        put(att, a, lanes, total, s)
+        put(att, a, lanes, total, s, old_att)
 
 
 def attention_backward(i, starts, ends, qkv, probs, att, datt, dqkv, gvec, width, rows):
@@ -148,6 +148,7 @@
     heads = jnp.where(group == lax.broadcasted_iota(jnp.int32, (8, width), 0), 1.0, 0.0).astype(BF16)
     both = att[pl.ds(a, WIN), :].astype(F32) * datt[pl.ds(a, WIN), :].astype(F32)
     high = both.astype(BF16)
+    old = dqkv[pl.ds(a, 16), :]
     delta = dot_nt(heads, high) + dot_nt(heads, (both - high.astype(F32)).astype(BF16))
     for pair in range(width // 128):
         lanes = slice(128 * pair, 128 * pair + 128)
@@ -170,33 +171,41 @@
             dk = dk_part if dk is None else dk + dk_part
             dq = dq_part if dq is None else dq + dq_part
         gvec[0:1, lanes] += colsum(dq * own) * scale
-        put(dqkv, a, lanes, dq * scale, s)
-        put(dqkv, a, klanes, dk, s)
-        put(dqkv, a, vlanes, dv, s)
+        put(dqkv, a, lanes, dq * scale, s, old)
+        put(dqkv, a, klanes, dk, s, old)
+        put(dqkv, a, vlanes, dv, s, old)
 
 
 def middle_kernel(
-    packs, start_in, end_in, qkv_in, qkvh_in, tok_in, tokh, cot_in, coth, wo, wu, wd, vec, upb,
-    out_hbm, dhid_hbm, dqkv_hbm, gvec, gupb, *refs,
+    packs, start_in, end_in, qkv_in, qkvh_in, tok_in, tokh, cot_in, coth, wqkv, wo, wu, wd, vec, upb, out_hbm, dx_hbm, *refs
 ):
+    first_hbm, second_hbm, first, second = (None,) * 4
     if packs:
-        packed_hbm, packed, *refs = refs
-    gwo, gwu, gwd, qkv, dqkv, probs, att, datt, tok, cot, out_buf, dhid_buf, starts, ends, sems = refs
+        first_hbm, second_hbm, first, second, *refs = refs
+        gsum, gupb, gwo, gwu, gwd, *refs = refs
+        gw = gwu.at[:, : 3 * wo.shape[0]]
+    else:
+        gsum, gupb, gw, gwo, gwu, gwd, *refs = refs
+    qkv, dqkv, probs, att, datt, tok, cot, out_buf, row_buf, starts, ends, sems = refs
     rows, width = tok_in.shape
     ff = wu.shape[1]
+    chunk = ff
     extent = rows + HALO
     tile = out_buf.shape[1]
-    chunk = 512
+    early = rows // 3
     copies = [
         pltpu.make_async_copy(qkvh_in.at[pl.ds(0, LEFT)], qkv.at[pl.ds(0, LEFT)], sems.at[0]),
-        pltpu.make_async_copy(qkv_in, qkv.at[pl.ds(LEFT, rows)], sems.at[1]),
-        pltpu.make_async_copy(qkvh_in.at[pl.ds(LEFT, RIGHT)], qkv.at[pl.ds(LEFT + rows, RIGHT)], sems.at[2]),
+        pltpu.make_async_copy(qkv_in.at[pl.ds(0, early)], qkv.at[pl.ds(LEFT, early)], sems.at[1]),
+    ]
+    rest = [
+        pltpu.make_async_copy(qkv_in.at[pl.ds(early, rows - early)], qkv.at[pl.ds(LEFT + early, rows - early)], sems.at[2]),
+        pltpu.make_async_copy(qkvh_in.at[pl.ds(LEFT, RIGHT)], qkv.at[pl.ds(LEFT + rows, RIGHT)], sems.at[3]),
     ]
     later = [
-        pltpu.make_async_copy(tok_in, tok, sems.at[3]),
-        pltpu.make_async_copy(cot_in, cot, sems.at[4]),
+        pltpu.make_async_copy(tok_in, tok, sems.at[4]),
+        pltpu.make_async_copy(cot_in, cot, sems.at[5]),
     ]
-    for c in copies + later:
+    for c in copies + rest + later:
         c.start()
 
     shift = LEFT - lax.axis_index(AXES) * rows
@@ -223,13 +232,20 @@
     for c in copies:
         c.wait()
 
+    assert 3 * LONGEST + WIN <= early and rows > 5 * LONGEST
+
     @pl.loop(0, count)
     def _(i):
+        @pl.when(i == 4)
+        def _():
+            for c in rest:
+                c.wait()
+
         attention_forward(i, starts, ends, qkv, probs, att, width)
 
-    bo, bd, g2, b2 = (vec[j : j + 1, :] for j in (2, 3, 6, 7))
-
-    def feed(x, c, at, own, sums):
+    bo, bd, g1, b1, g2, b2 = (vec[j : j + 1, :] for j in (2, 3, 4, 5, 6, 7))
+
+    def feed(x, c, at, own):
         hid = x.astype(F32) + dot(at, wo[...]) + bo
         xhat, inverse = normed(hid)
         n2 = (xhat * g2 + b2).astype(BF16)
@@ -258,94 +274,133 @@
         if own:
             gwo[...] += dot_tn(at, dhid_b)
             for j, x in ((2, dhid), (3, c.astype(F32)), (6, dn2 * xhat), (7, dn2)):
-                gvec[j : j + 1, :] += colsum(x)
+                gsum[j : j + 1, :] += colsum(x)
             return hid + down + bd, dhid, da
         return da
 
     gwo[...] = jnp.zeros_like(gwo)
     gwu[...] = jnp.zeros_like(gwu)
     gwd[...] = jnp.zeros_like(gwd)
-    gvec[...] = jnp.zeros_like(gvec)
+    gsum[...] = jnp.zeros_like(gsum)
     gupb[...] = jnp.zeros_like(gupb)
     for c in later:
         c.wait()
 
-    def writes(i, slot):
-        at = pl.ds(pl.multiple_of(i * tile, tile), tile)
-        return (
-            pltpu.make_async_copy(out_buf.at[slot], out_hbm.at[at], sems.at[5 + slot]),
-            pltpu.make_async_copy(dhid_buf.at[slot], dhid_hbm.at[at], sems.at[7 + slot]),
-        )
-
-    @pl.loop(0, rows // tile)
+    def tile_at(i):
+        return pl.ds(pl.multiple_of(i * tile, tile), tile)
+
+    def layer_write(i):
+        return pltpu.make_async_copy(out_buf.at[i % 2], out_hbm.at[tile_at(i)], sems.at[6 + i % 2])
+
+    def row_write(i, first_slot):
+        slot = first_slot + i % 2
+        return pltpu.make_async_copy(row_buf.at[slot], dx_hbm.at[tile_at(i)], sems.at[8 + slot])
+
+    def row_read(i):
+        return pltpu.make_async_copy(dx_hbm.at[tile_at(i)], row_buf.at[i % 2], sems.at[12 + i % 2])
+
+    tiles = rows // tile
+
+    @pl.loop(0, tiles)
     def _(i):
-        slot = i % 2
         at = pl.multiple_of(i * tile, tile)
         here = pl.ds(pl.multiple_of(LEFT + at, 16), tile)
-        layer, dhid, da = feed(tok[pl.ds(at, tile), :], cot[pl.ds(at, tile), :], att[here, :], True, None)
+        layer, dhid, da = feed(tok[pl.ds(at, tile), :], cot[pl.ds(at, tile), :], att[here, :], True)
         datt[here, :] = da
 
         @pl.when(i >= 2)
         def _():
-            for w in writes(i - 2, slot):
-                w.wait()
-
-        out_buf[slot] = layer.astype(BF16)
-        dhid_buf[slot] = dhid
-        for w in writes(i, slot):
-            w.start()
+            layer_write(i - 2).wait()
+            row_write(i - 2, 0).wait()
+
+        out_buf[i % 2] = layer.astype(BF16)
+        row_buf[i % 2] = dhid
+        layer_write(i).start()
+        row_write(i, 0).start()
 
     sides = jnp.concatenate([att[pl.ds(0, LEFT), :], att[pl.ds(LEFT + rows, RIGHT), :]], axis=0)
-    da = feed(tokh[...], coth[...], sides, False, None)
+    da = feed(tokh[...], coth[...], sides, False)
     datt[pl.ds(0, LEFT), :] = da[:LEFT]
     datt[pl.ds(LEFT + rows, RIGHT), :] = da[LEFT:]
 
     if packs:
 
-        @pl.loop(0, packed.shape[0] // 4)
+        @pl.loop(0, second.shape[0] // 4)
         def _(i):
-            pack_second(i, gwo, gwu, packed)
-
-        pack_down(gwd, packed)
-        sent = pltpu.make_async_copy(packed, packed_hbm, sems.at[10])
-        sent.start()
+            pack_second(i, gwo, gwu, second)
+
+        pack_down(gwd, second)
+        second_sent = pltpu.make_async_copy(second, second_hbm, sems.at[14])
+        second_sent.start()
+
+    for i in (tiles - 2, tiles - 1):
+        row_write(i, 0).wait()
+    row_read(0).start()
+    gw[...] = jnp.zeros(gw.shape, F32)
 
     @pl.loop(0, count)
     def _(i):
-        attention_backward(i, starts, ends, qkv, probs, att, datt, dqkv, gvec, width, rows)
-
-    last = pltpu.make_async_copy(dqkv.at[pl.ds(LEFT, rows)], dqkv_hbm, sems.at[9])
-    last.start()
-    n = rows // tile
-    for i in range(max(n - 2, 0), n):
-        for w in writes(i, i % 2):
-            w.wait()
-    last.wait()
+        attention_backward(i, starts, ends, qkv, probs, att, datt, dqkv, gsum, width, rows)
+
+    @pl.loop(0, tiles)
+    def _(i):
+        at = pl.multiple_of(i * tile, tile)
+        row_read(i).wait()
+
+        @pl.when(i + 1 < tiles)
+        def _():
+            row_read(i + 1).start()
+
+        @pl.when(i >= 2)
+        def _():
+            row_write(i - 2, 2).wait()
+
+        d = dqkv[pl.ds(pl.multiple_of(LEFT + at, 16), tile), :]
+        xhat, inverse = normed(tok[pl.ds(at, tile), :].astype(F32))
+        n1 = (xhat * g1 + b1).astype(BF16)
+        gw[...] += dot(n1.T, d)
+        dn1 = dot_nt(d, wqkv[...])
+        for j, x in ((1, d[:, 2 * width :].astype(F32)), (4, dn1 * xhat), (5, dn1)):
+            gsum[j : j + 1, :] += colsum(x)
+        row_buf[2 + i % 2] = row_buf[i % 2] + norm_back(dn1, xhat, inverse, g1)
+        row_write(i, 2).start()
+
     if packs:
-        sent.wait()
-
-
-def middle(packs, start, end, qkv, qkvh, tok, tokh, cot, coth, wo, wu, wd, vec, upb):
+
+        @pl.loop(0, first.shape[0] // 4)
+        def _(i):
+            pack_first(i, gw, first)
+
+        pack_small(gsum[...], gupb[...], first)
+        first_sent = pltpu.make_async_copy(first, first_hbm, sems.at[15])
+        first_sent.start()
+        first_sent.wait()
+        second_sent.wait()
+    for i in (tiles - 2, tiles - 1):
+        layer_write(i).wait()
+        row_write(i, 2).wait()
+
+
+def middle(packs, start, end, qkv, qkvh, tok, tokh, cot, coth, wqkv, wo, wu, wd, vec, upb):
     rows, width = tok.shape
     ff = wu.shape[1]
-    padded = rows + HALO + WIN
-    tile = 256
+    padded = rows + HALO + SPARE
+    tile = 512
     vmem = pl.BlockSpec(memory_space=pltpu.VMEM)
     smem = pl.BlockSpec(memory_space=pltpu.SMEM)
     anyw = pl.BlockSpec(memory_space=pl.ANY)
     most = rows // SHORTEST + 4
     n = lax.axis_size(AXES)
     S = jax.ShapeDtypeStruct
-    sums = [((width, width), F32), ((width, ff), F32), ((width, ff), F32)]
-    slabs = (n, 16, SECOND)
+    sums = [((8, width), F32), ((8, ff), F32), ((width, 3 * width), F32), ((width, width), F32), ((width, ff), F32), ((width, ff), F32)]
+    slabs = [((n, 16, FIRST), BF16), ((n, 16, SECOND), BF16)]
+    held = slabs + [a for i, a in enumerate(sums) if i != 2] if packs else []
     return pl.pallas_call(
         functools.partial(middle_kernel, packs),
-        out_shape=[
-            S((rows, width), BF16), S((rows, width), F32), S((rows, 3 * width), BF16), S((8, width), F32), S((8, ff), F32),
-        ] + ([S(slabs, BF16)] if packs else [S(*a) for a in sums]),
-        in_specs=[smem, smem, anyw, anyw, anyw, vmem, anyw, vmem, vmem, vmem, vmem, vmem, vmem],
-        out_specs=[anyw, anyw, anyw, vmem, vmem] + ([anyw] if packs else [vmem] * 3),
-        scratch_shapes=([pltpu.VMEM(slabs, BF16)] + [pltpu.VMEM(*a) for a in sums] if packs else [])
+        out_shape=[S((rows, width), BF16), S((rows, width), F32)] + [S(*a) for a in (slabs if packs else sums)],
+        in_specs=[smem, smem, anyw, anyw, anyw, vmem, anyw] + [vmem] * 7,
+        out_specs=[anyw, anyw] + ([anyw] * 2 if packs else [vmem] * 6),
+        scratch_shapes=[pltpu.VMEM(*a) for a in held]
         + [
             pltpu.VMEM((padded, 3 * width), BF16),
             pltpu.VMEM((padded, 3 * width), BF16),
@@ -355,66 +410,14 @@
             pltpu.VMEM((rows, width), BF16),
             pltpu.VMEM((rows, width), BF16),
             pltpu.VMEM((2, tile, width), BF16),
-            pltpu.VMEM((2, tile, width), F32),
+            pltpu.VMEM((4, tile, width), F32),
             pltpu.SMEM((most,), jnp.int32),
             pltpu.SMEM((most,), jnp.int32),
-            pltpu.SemaphoreType.DMA((11,)),
+            pltpu.SemaphoreType.DMA((16,)),
         ],
         compiler_params=pltpu.CompilerParams(vmem_limit_bytes=VMEM_BYTES),
         name="middle",
-    )(start, end, qkv, qkvh, tok, tokh, cot, coth, wo, wu, wd, vec, upb)
-
-
-def last_kernel(packs, tok, dhid, dqkv, weight, vec, gvec, gupb, dx, *refs):
-    packed, gw, sums = refs if packs else (None,) + refs
-    width = tok.shape[1]
-
-    @pl.when(pl.program_id(0) == 0)
-    def _():
-        gw[...] = jnp.zeros_like(gw)
-        sums[...] = gvec[...]
-
-    gain, shift = vec[4:5, :], vec[5:6, :]
-    xhat, inverse = normed(tok[...].astype(F32))
-    n1 = (xhat * gain + shift).astype(BF16)
-    d = dqkv[...]
-    gw[...] += dot_tn(n1, d)
-    dn1 = dot_nt(d, weight[...])
-    sums[1:2, :] += colsum(d[:, 2 * width :].astype(F32))
-    sums[4:5, :] += colsum(dn1 * xhat)
-    sums[5:6, :] += colsum(dn1)
-    dx[...] = dhid[...] + norm_back(dn1, xhat, inverse, gain)
-
-    if packs:
-
-        @pl.when(pl.program_id(0) == pl.num_programs(0) - 1)
-        def _():
-            @pl.loop(0, packed.shape[0] // 4)
-            def _(i):
-                pack_first(i, gw, packed)
-
-            pack_small(sums[...], gupb[...], packed)
-
-
-def last(packs, tok, dhid, dqkv, weight, vec, gvec, gupb):
-    rows, width = tok.shape
-    wide = weight.shape[1]
-    tile = 512
-    n = lax.axis_size(AXES)
-    whole = lambda a: pl.BlockSpec(a, lambda i: (0,) * len(a))
-    rowed = lambda n: pl.BlockSpec((tile, n), lambda i: (i, 0))
-    S = jax.ShapeDtypeStruct
-    sums = [(width, wide), (8, width)]
-    return pl.pallas_call(
-        functools.partial(last_kernel, packs),
-        grid=(rows // tile,),
-        out_shape=[S((rows, width), F32)] + ([S((n, 16, FIRST), BF16)] if packs else [S(a, F32) for a in sums]),
-        in_specs=[rowed(width), rowed(width), rowed(wide)] + [whole(a.shape) for a in (weight, vec, gvec, gupb)],
-        out_specs=[rowed(width)] + ([whole((n, 16, FIRST))] if packs else [whole(a) for a in sums]),
-        scratch_shapes=[pltpu.VMEM(a, F32) for a in sums] if packs else [],
-        compiler_params=pltpu.CompilerParams(vmem_limit_bytes=VMEM_BYTES),
-        name="last",
-    )(tok, dhid, dqkv, weight, vec, gvec, gupb)
+    )(start, end, qkv, qkvh, tok, tokh, cot, coth, wqkv, wo, wu, wd, vec, upb)
 
 
 COLS, ROWS_UP, LAYERS, CORES = 2, 2, 4, 2
@@ -747,7 +750,7 @@
         self.move(ref, ref, self.core_sem.at[self.share, 0], place(self.x, self.c, self.z, self.y)).wait_send()
 
 
-def scatter_kernel(first_in, second_in, gqkv, gwo, gwu, gwd, small, mine, core, first, second, third, *sems):
+def scatter_kernel(first_in, second_in, one, two, mine, core, first, second, third, *sems):
     x, c, z, y = here()
     greet(
         [place(x, c, lax.rem(z + d, LAYERS), y) for d in range(1, LAYERS)]
@@ -759,32 +762,44 @@
     for n in range(3):
         for s in shares:
             s.level(n)
-    two, one = jnp.concatenate([s.result() for s in shares[:2]], axis=1), jnp.concatenate([s.result() for s in shares[2:]], axis=1)
-    width = gwo.shape[1]
-    gqkv[:, :SPARE_QKV] = one[:12, 128:]
-    gwo[...] = two[:12, :width]
-    gwu[:, :SPARE_UP] = two[:12, width:DOWN_AT]
-    for j in range(3):
-        gqkv[4 * j : 4 * j + 4, SPARE_QKV:] = one[12:, 128 + 256 * j : 128 + 256 * (j + 1)]
-        gwu[4 * j : 4 * j + 4, SPARE_UP:] = two[12:, width * j : width * (j + 1)]
-        gwd[16 * j : 16 * j + 16, :] = two[:, DOWN_AT + width * j : DOWN_AT + width * (j + 1)]
-    small[...] = one[:, :128]
+    for s in shares:
+        (two if s.block else one)[:, s.lanes] = s.result()
     for s in shares:
         s.finish()
 
 
-def scatter_all(first, second, width, ff):
-    n = first.shape[0]
+def finish_kernel(one, two, gqkv, gwo, gwu, gwd, ups, *smalls):
+    width, own = gwo.shape[1], gwo.shape[0]
+    gqkv[:, :SPARE_QKV] = one[:own, 128:]
+    gwo[...] = two[:own, :width]
+    gwu[:, :SPARE_UP] = two[:own, width:DOWN_AT]
+    for j in range(3):
+        gqkv[4 * j : 4 * j + 4, SPARE_QKV:] = one[own:, 128 + 256 * j : 128 + 256 * (j + 1)]
+        gwu[4 * j : 4 * j + 4, SPARE_UP:] = two[own:, width * j : width * (j + 1)]
+        gwd[16 * j : 16 * j + 16, :] = two[:, DOWN_AT + width * j : DOWN_AT + width * (j + 1)]
+    ups[...] = one[8, : ups.shape[0]]
+    for j, ref in enumerate(smalls):
+        ref[...] = one[j, :own]
+
+
+def finish(one, two, width, ff):
+    n = lax.axis_size(AXES)
+    own = width // n
+    S = jax.ShapeDtypeStruct
+    shapes = [(own, 3 * width), (own, width), (own, ff), (ff // n, width), (ff // n,)] + [(own,)] * 8
+    return pl.pallas_call(finish_kernel, out_shape=[S(a, F32) for a in shapes], name="finish")(one, two)
+
+
+def scatter_all(first, second):
     vmem = pl.BlockSpec(memory_space=pltpu.VMEM)
     S = jax.ShapeDtypeStruct
-    own = width // n
     k = len(SHARES)
     widest = max(hi - lo for _, lo, hi, _ in SHARES)
     return pl.pallas_call(
         scatter_kernel,
-        out_shape=(S((own, 3 * width), F32), S((own, width), F32), S((own, ff), F32), S((ff // n, width), F32), S((16, 128), F32)),
+        out_shape=(S((16, FIRST), F32), S((16, SECOND), F32)),
         in_specs=[vmem, vmem],
-        out_specs=(vmem,) * 5,
+        out_specs=(vmem,) * 2,
         scratch_shapes=[
             pltpu.VMEM((k, 16, 16, widest), BF16),
             pltpu.VMEM((k, 16, 16, widest), BF16),
@@ -828,17 +843,15 @@
         side = lambda a: jnp.concatenate([lax.ppermute(a[a.shape[0] - LEFT :], AXES, up), lax.ppermute(a[:RIGHT], AXES, down)])
         tokh, coth = side(tokens), side(cotangent)
     qkv, qkvh = project(tokens, tokh, wqkv, vec)
-    layer, dhid, dqkv, gvec, gupb, *grads = middle(
-        packs, image_start, image_end, qkv, qkvh, tokens, tokh, cotangent, coth, wo, wu, wd, vec, upb
+    layer, dx, *grads = middle(
+        packs, image_start, image_end, qkv, qkvh, tokens, tokh, cotangent, coth, wqkv, wo, wu, wd, vec, upb
     )
-    dx, *grads1 = last(packs, tokens, dhid, dqkv, wqkv, vec, gvec, gupb)
     if packs:
-        gqkv, gwo, gwu, gwd, sums = scatter_all(grads1[0], grads[0], width, ff)
-        sums, ups = sums[:8, : q_bias.shape[0]], sums[8, : up_bias.shape[0]]
+        gqkv, gwo, gwu, gwd, ups, *sums = finish(*scatter_all(*grads), width, ff)
     else:
         reduced = lambda a: lax.psum_scatter(a, AXES, scatter_dimension=0, tiled=True)
-        gqkv, gwo, gwu, gwd = (reduced(a) for a in (grads1[0], grads[0], grads[1], grads[2].T))
-        sums, ups = reduced(grads1[1].T).T, reduced(gupb[0])
+        sums, ups = reduced(grads[0].T).T, reduced(grads[1][0])
+        gqkv, gwo, gwu, gwd = (reduced(a) for a in (grads[2], grads[3], grads[4], grads[5].T))
     return (
         layer, dx, gqkv, sums[0], sums[1], gwo, sums[2], gwu, ups, gwd, sums[3], sums[4], sums[5], sums[6], sums[7],
     )

time: 216 us -> 194 us (0.90)
  Pallas kernels: 203 us -> 191 us
  local copies, waits for them, and re-layouts: 9.42 us -> 0.8 us
    pallas_call x2, Pallas kernels: 51.4 us -> 37.8 us  [the longest x1 36.1 us: scatter_all(): pl.pallas_call(scatter_kernel, out_shape=(S((16, FIRST), F32), S((16, SEC...]
    unnamed x4 -> x0, local copies, waits for them, and re-layouts: 5.93 us -> none
    squeeze x2 -> x0, local copies, waits for them, and re-layouts: 2.7 us -> none  [the longest x1 1.51 us: per_device(): sums[7]]
where the time goes in v2:
time: 194 us
  Pallas kernels  191 us (98%)
    pallas_call x1, Pallas kernels, middle(): pl.pallas_call(functools.partial(middle_kernel, packs), out_shape=[S((row...  103 us
    pallas_call x1, Pallas kernels, gather_all(): pl.pallas_call(gather_kernel, out_shape=(S((width, wqkv.shape[1]), BF16),...  39.8 us
    pallas_call x1, Pallas kernels, scatter_all(): pl.pallas_call(scatter_kernel, out_shape=(S((16, FIRST), F32), S((16, SEC...  36.1 us
    pallas_call x1, Pallas kernels, project(): pl.pallas_call(qkv_kernel, grid=(rows // tile,), out_shape=(jax.ShapeDtyp...  10 us

profile of v2, /device:TPU:0, one launch (start us, length us, event | category | flops | bytes accessed | tf_op | source)
XLA Modules:
  0.0 194.0 jit_solution(3789956022346220152)
XLA Ops:
  0.6 0.8 stack.35
  1.4 1.3 fusion.2.small
  2.7 39.8 %gather.1 = (bf16[384,1152]{1,0:T(8,128)(2,1)}, bf16[384,384]{1,0:T(8,128)(2,1)}, bf16[384,1536]{1,0:T(8,128)(2,1)}, bf16[1536,384]{1,0:T(8,128)(2,1)}, f32[8,38...) custom-call(bf16[16,128]{1,0:T(8,128)(2,1)} %fusion.2.small, ...), custom_call_target="tpu_custom_call" | custom-call | tf_op jit(solution)/shard_map/gather/pallas_call | solution.py:605
  42.5 10.0 %project.1 = (bf16[3072,1152]{1,0:T(8,128)(2,1)}, bf16[272,1152]{1,0:T(8,128)(2,1)}) custom-call(bf16[3072,384]{1,0:T(8,128)(2,1)} %tok_in.1, bf16[272,384]{1,0:T(8,128)(2,1)} %get-tuple-element.44.tokh, bf16[384,1152]{1,0:T(8,128)(2,1)} %get-tuple-element.45.weight.wqkv, f32[8,384]{1,0:T(8,128)} %get-tuple-element.46.vec), custom_call_target="tpu_custom_call" | custom-call | tf_op jit(solution)/shard_map/project/pallas_call | solution.py:81
  52.5 103.4 %middle.1 = (bf16[3072,384]{1,0:T(8,128)(2,1)}, f32[3072,384]{1,0:T(8,128)}, bf16[32,16,1024]{2,1,0:T(8,128)(2,1)}, bf16[32,16,2688]{2,1,0:T(8,128)(2,1)}) custom-call(s32[3072]{0:T(1024)} %start_in.1, s32[3072]{0:T(1024)} %end_in.1, bf16[3072,1152]{1,0:T(8,128)(2,1)} %get-tuple-element.47.qkv_in, bf16[272,1152]{1,0:T(8,128)(2,1)} %get-tuple-element.48.qkvh_in, ...), custom_call_target="tpu_custom_call" | custom-call | tf_op jit(solution)/shard_map/middle/pallas_call | solution.py:398
  156.0 36.1 %scatter.1 = (f32[16,1024]{1,0:T(8,128)}, f32[16,2688]{1,0:T(8,128)}) custom-call(bf16[32,16,1024]{2,1,0:T(8,128)(2,1)} %get-tuple-element.56.first_in, bf16[32,16,2688]{2,1,0:T(8,128)(2,1)} %get-tuple-element.57.second_in), custom_call_target="tpu_custom_call" | custom-call | tf_op jit(solution)/shard_map/scatter/pallas_call | solution.py:798
  192.1 1.7 finish.1

commit v3 on v2

--- a/solution.py
+++ b/solution.py
@@ -423,7 +423,8 @@
 COLS, ROWS_UP, LAYERS, CORES = 2, 2, 4, 2
 LANES = 3584
 SMALL, QKV, OUT, UP, DOWN = 0, 128, 1280, 1664, 2432
-PIECES = ((0, 640, 0), (640, 1280, 1), (1280, 2432, 0), (2432, 3584, 1))
+SPLIT = 768
+PIECES = ((0, 1280, 1), (1280, 2176, 1), (2176, 3072, 1), (3072, 3584, 0))
 MESH = pl.DeviceIdType.MESH
 
 
@@ -517,72 +518,30 @@
         remote(ref, ref, self.send.at[piece], self.recv.at[piece, 0], place(self.x, self.c, self.z, self.y)).wait_send()
 
 
-def gather_kernel(
-    small, wqkv_in, wo_in, wu_in, wd_in, tok, cot,
-    wqkv, wo, wu, wd, vec, upb, tokh, coth,
-    slabs, send, recv, side_send, side_recv,
-):
-    x, c, z, y = here()
-    me = number(x, c, z, y)
-    rows, width = tok.shape
-    n = slabs.shape[0]
-    own = slabs.at[me]
-    own[:, SMALL:QKV] = small[...]
-    split = 768
-    up = wu_in[...].astype(F32)
-    top = jnp.concatenate([wqkv_in[...].astype(F32), wo_in[...].astype(F32), up[:, :split]], axis=1)
-    rest = jnp.concatenate([up[4 * i : 4 * i + 4, split:] for i in range(3)], axis=1)
-    own[:, QKV:DOWN] = jnp.concatenate([top, rest], axis=0).astype(BF16)
-    for i in range(3):
-        own[:, DOWN + width * i : DOWN + width * (i + 1)] = wd_in[16 * i : 16 * i + 16, :]
-
-    greet(
-        [place(x, c, lax.rem(z + d, LAYERS), y) for d in range(1, LAYERS)]
-        + [place(1 - x, c, z, y), place(x, c, z, 1 - y), place(x, 1 - c, z, y), along(1), along(-1)]
-    )
-    g = Gather(slabs, send, recv)
-    for p in (0, 1):
-        g.own(p)
-    sides = []
-    for j, (src, dst) in enumerate(((tok, tokh), (cot, coth))):
-        sides.append(remote(src.at[pl.ds(rows - LEFT, LEFT)], dst.at[pl.ds(0, LEFT)], side_send.at[2 * j], side_recv.at[2 * j], along(1)))
-        sides.append(remote(src.at[pl.ds(0, RIGHT)], dst.at[pl.ds(LEFT, RIGHT)], side_send.at[2 * j + 1], side_recv.at[2 * j + 1], along(-1)))
-    for p in (0, 1):
-        g.stage(p, 0)
-    for p in (2, 3):
-        g.own(p)
-    for s in sides:
-        s.start()
-    for level in (1, 2):
-        for p in (0, 1):
-            g.stage(p, level)
-    for level in (0, 1, 2):
-        for p in (2, 3):
-            g.stage(p, level)
-    for p in range(4):
-        g.siblings(p)
-    for s in sides:
-        s.wait()
-    for p in range(4):
-        g.finish(p)
-
-    @pl.loop(0, n // 4)
-    def _(i):
-        at = pl.ds(pl.multiple_of(48 * i, 16), 48)
-        parts = [slabs[4 * i + d, :, QKV:DOWN].astype(F32) for d in range(4)]
-        full = jnp.concatenate([p[:12] for p in parts], axis=0).astype(BF16)
-        wqkv[at, :] = full[:, : OUT - QKV]
-        wo[at, :] = full[:, OUT - QKV : UP - QKV]
-        wu[at, :split] = full[:, UP - QKV :]
-        wu[at, split:] = jnp.concatenate([p[12:, split * j : split * (j + 1)] for p in parts for j in range(3)], axis=0).astype(BF16)
-        for d in range(4):
-            for j in range(3):
-                wd[pl.ds(pl.multiple_of(48 * (4 * i + d) + 16 * j, 16), 16), :] = slabs[4 * i + d, :, DOWN + width * j : DOWN + width * (j + 1)]
-
+def unpack_first(i, slabs, wqkv):
+    parts = [slabs[4 * i + d, :12, QKV:OUT].astype(F32) for d in range(4)]
+    wqkv[pl.ds(pl.multiple_of(48 * i, 16), 48), :] = jnp.concatenate(parts, axis=0).astype(BF16)
+
+
+def unpack_rest(i, slabs, wo, wu, wd):
+    width, split = wo.shape[1], SPLIT
+    at = pl.ds(pl.multiple_of(48 * i, 16), 48)
+    parts = [slabs[4 * i + d, :, OUT:DOWN].astype(F32) for d in range(4)]
+    full = jnp.concatenate([p[:12] for p in parts], axis=0).astype(BF16)
+    wo[at, :] = full[:, : UP - OUT]
+    wu[at, :split] = full[:, UP - OUT :]
+    spare = [slabs[4 * i + d, :, QKV:DOWN].astype(F32)[12:] for d in range(4)]
+    wu[at, split:] = jnp.concatenate([p[:, split * j : split * (j + 1)] for p in spare for j in range(3)], axis=0).astype(BF16)
+    for d in range(4):
+        for j in range(3):
+            wd[pl.ds(pl.multiple_of(48 * (4 * i + d) + 16 * j, 16), 16), :] = slabs[4 * i + d, :, DOWN + width * j : DOWN + width * (j + 1)]
+
+
+def unpack_small(slabs, vec, upb):
     lane = lax.broadcasted_iota(jnp.int32, (8, 128), 1)
-    lines = [jnp.zeros((8, 128), F32) for _ in range(width // 128)]
+    lines = [jnp.zeros((8, 128), F32) for _ in range(vec.shape[1] // 128)]
     ups = [jnp.zeros((8, 128), F32) for _ in range(upb.shape[1] // 128)]
-    for k in range(n):
+    for k in range(slabs.shape[0]):
         s = slabs[k, :, SMALL:QKV].astype(F32)
         for tiles, block, size in ((lines, s[:8], 12), (ups, s[8:], 48)):
             t, by = divmod(size * k, 128)
@@ -596,6 +555,94 @@
     upb[...] = jnp.concatenate(ups, axis=1)
 
 
+def gather_kernel(
+    small, wqkv_in, wo_in, wu_in, wd_in, tok, cot,
+    wqkv, wo, wu, wd, vec, upb, tokh, coth, qkv, qkvh,
+    slabs, tok_v, tokh_v, tile_v, send, recv, side_send, side_recv, sems,
+):
+    x, c, z, y = here()
+    me = number(x, c, z, y)
+    rows, width = tok.shape
+    n = slabs.shape[0]
+    load = pltpu.make_async_copy(tok, tok_v, sems.at[0])
+    load.start()
+    own = slabs.at[me]
+    own[:, SMALL:QKV] = small[...]
+    up = wu_in[...].astype(F32)
+    top = jnp.concatenate([wqkv_in[...].astype(F32), wo_in[...].astype(F32), up[:, :SPLIT]], axis=1)
+    rest = jnp.concatenate([up[4 * i : 4 * i + 4, SPLIT:] for i in range(3)], axis=1)
+    own[:, QKV:DOWN] = jnp.concatenate([top, rest], axis=0).astype(BF16)
+    for i in range(3):
+        own[:, DOWN + width * i : DOWN + width * (i + 1)] = wd_in[16 * i : 16 * i + 16, :]
+
+    greet(
+        [place(x, c, lax.rem(z + d, LAYERS), y) for d in range(1, LAYERS)]
+        + [place(1 - x, c, z, y), place(x, c, z, 1 - y), place(x, 1 - c, z, y), along(1), along(-1)]
+    )
+    g = Gather(slabs, send, recv)
+    g.own(0)
+    sides = []
+    for j, (src, dst) in enumerate(((tok, tokh_v), (cot, coth))):
+        sides.append(remote(src.at[pl.ds(rows - LEFT, LEFT)], dst.at[pl.ds(0, LEFT)], side_send.at[2 * j], side_recv.at[2 * j], along(1)))
+        sides.append(remote(src.at[pl.ds(0, RIGHT)], dst.at[pl.ds(LEFT, RIGHT)], side_send.at[2 * j + 1], side_recv.at[2 * j + 1], along(-1)))
+    for p in (1, 2, 3):
+        g.own(p)
+    for p in range(4):
+        g.stage(p, 0)
+    g.stage(0, 1)
+    for s in sides:
+        s.start()
+    for p in (1, 2, 3):
+        g.stage(p, 1)
+    g.stage(0, 2)
+    g.siblings(0)
+
+    @pl.loop(0, n // 4)
+    def _(i):
+        unpack_first(i, slabs, wqkv)
+
+    unpack_small(slabs, vec, upb)
+    load.wait()
+    tile = tile_v.shape[1]
+
+    def write(i):
+        return pltpu.make_async_copy(tile_v.at[i % 2], qkv.at[pl.ds(tile * i, tile)], sems.at[1 + i % 2])
+
+    gain, shift = vec[4:5, :], vec[5:6, :]
+    bias = jnp.concatenate([vec[0:1, :], jnp.zeros((1, width), F32), vec[1:2, :]], axis=1)
+    steps = [lambda p=p: g.stage(p, 2) for p in (1, 2, 3)]
+    for i in range(rows // tile):
+        if i < len(steps):
+            steps[i]()
+        if i >= 2:
+            write(i - 2).wait()
+        tile_v[i % 2] = qkv_rows(tok_v[pl.ds(tile * i, tile), :], wqkv[...], gain, shift, bias, width)
+        write(i).start()
+    for p in (1, 2, 3):
+        g.siblings(p)
+
+    @pl.loop(0, n // 4)
+    def _(i):
+        unpack_rest(i, slabs, wo, wu, wd)
+
+    for s in sides:
+        s.wait()
+    last = rows // tile
+    write(last - 2).wait()
+    tile_v[last % 2, :HALO] = qkv_rows(tokh_v[...], wqkv[...], gain, shift, bias, width)
+    ends = [
+        pltpu.make_async_copy(tile_v.at[last % 2, pl.ds(0, HALO)], qkvh, sems.at[3]),
+        pltpu.make_async_copy(tokh_v, tokh, sems.at[4]),
+    ]
+    for e in ends:
+        e.start()
+    for p in range(4):
+        g.finish(p)
+    write(last - 1).wait()
+    for e in ends:
+        e.wait()
+
+
 def gather_all(small, wqkv, wo, wu, wd, tok, cot):
     n = lax.axis_size(AXES)
     rows, width = tok.shape
@@ -607,15 +654,20 @@
         out_shape=(
             S((width, wqkv.shape[1]), BF16), S((width, width), BF16), S((width, wu.shape[1]), BF16), S((wd.shape[0] * n, width), BF16),
             S((8, width), F32), S((8, wu.shape[1]), F32), S((HALO, width), BF16), S((HALO, width), BF16),
+            S((rows, wqkv.shape[1]), BF16), S((HALO, wqkv.shape[1]), BF16),
         ),
         in_specs=[vmem] * 5 + [anyw] * 2,
-        out_specs=(vmem,) * 6 + (anyw,) * 2,
+        out_specs=(vmem,) * 6 + (anyw,) * 4,
         scratch_shapes=[
             pltpu.VMEM((n, 16, LANES), BF16),
+            pltpu.VMEM((rows, width), BF16),
+            pltpu.VMEM((HALO, width), BF16),
+            pltpu.VMEM((2, 512, wqkv.shape[1]), BF16),
             pltpu.SemaphoreType.DMA((4,)),
             pltpu.SemaphoreType.DMA((4, n)),
             pltpu.SemaphoreType.DMA((4,)),
             pltpu.SemaphoreType.DMA((4,)),
+            pltpu.SemaphoreType.DMA((5,)),
         ],
         compiler_params=pltpu.CompilerParams(collective_id=0, has_side_effects=True, vmem_limit_bytes=VMEM_BYTES),
         name="gather",
@@ -625,7 +677,9 @@
 FIRST, SECOND = 1024, 2688
 SPARE_QKV, SPARE_UP = 896, 1152
 DOWN_AT = 1536
-SHARES = ((1, 0, 1408, 0), (1, 1408, 2688, 1), (0, 0, 512, 0), (0, 512, 1024, 1))
+SHARES = (
+    (1, 0, 512, 0), (1, 512, 1024, 1), (1, 1024, 1408, 0), (1, 1408, 1792, 1), (1, 1792, 2304, 0), (1, 2304, 2688, 1), (0, 0, 512, 0), (0, 512, 1024, 1),
+)
 
 
 def pack_first(i, gw, out):
@@ -759,9 +813,12 @@
     shares = [Scatter(i, (first_in, second_in), mine, core, first, second, third, sems) for i in range(len(SHARES))]
     for s in shares:
         s.begin()
-    for n in range(3):
-        for s in shares:
-            s.level(n)
+    pairs = len(shares) // 2
+    for step in range(pairs + 2):
+        for n in range(3):
+            if 0 <= step - n < pairs:
+                for s in shares[2 * (step - n) : 2 * (step - n) + 2]:
+                    s.level(n)
     for s in shares:
         (two if s.block else one)[:, s.lanes] = s.result()
     for s in shares:
@@ -832,7 +889,9 @@
     packs = lax.axis_size("dp") == COLS * CORES and lax.axis_size("fsdp") == LAYERS * ROWS_UP
     if packs:
         small = small_parameters(vectors, up_bias)
-        wqkv, wo, wu, wd, vec, upb, tokh, coth = gather_all(small, qkv_weight, out_weight, up_weight, down_weight, tokens, cotangent)
+        wqkv, wo, wu, wd, vec, upb, tokh, coth, qkv, qkvh = gather_all(
+            small, qkv_weight, out_weight, up_weight, down_weight, tokens, cotangent
+        )
     else:
         whole = lambda a: lax.all_gather(a, AXES, axis=0, tiled=True)
         wqkv, wo, wu, wd = (whole(a) for a in (qkv_weight, out_weight, up_weight, down_weight))
@@ -842,7 +901,7 @@
         up, down = [(i, i + 1) for i in range(n - 1)], [(i + 1, i) for i in range(n - 1)]
         side = lambda a: jnp.concatenate([lax.ppermute(a[a.shape[0] - LEFT :], AXES, up), lax.ppermute(a[:RIGHT], AXES, down)])
         tokh, coth = side(tokens), side(cotangent)
-    qkv, qkvh = project(tokens, tokh, wqkv, vec)
+        qkv, qkvh = project(tokens, tokh, wqkv, vec)
     layer, dx, *grads = middle(
         packs, image_start, image_end, qkv, qkvh, tokens, tokh, cotangent, coth, wqkv, wo, wu, wd, vec, upb
     )

time: 194 us -> 182 us (0.938)
  Pallas kernels: 191 us -> 179 us
    pallas_call x1 -> x0, Pallas kernels: 10 us -> none  [project(): pl.pallas_call(qkv_kernel, grid=(rows // tile,), out_shape=(jax.ShapeDtyp...]
    pallas_call x1, Pallas kernels: 36.1 us -> 33.8 us  [scatter_all(): pl.pallas_call(scatter_kernel, out_shape=(S((16, FIRST), F32), S((16, SEC...]
where the time goes in v3:
time: 182 us
  Pallas kernels  179 us (98%)
    pallas_call x1, Pallas kernels, middle(): pl.pallas_call(functools.partial(middle_kernel, packs), out_shape=[S((row...  103 us
    pallas_call x1, Pallas kernels, gather_all(): pl.pallas_call(gather_kernel, out_shape=(S((width, wqkv.shape[1]), BF16),...  40 us
    pallas_call x1, Pallas kernels, scatter_all(): pl.pallas_call(scatter_kernel, out_shape=(S((16, FIRST), F32), S((16, SEC...  33.8 us

profile of v3, /device:TPU:0, one launch (start us, length us, event | category | flops | bytes accessed | tf_op | source)
XLA Modules:
  0.0 181.8 jit_solution(614759084421737863)
XLA Ops:
  0.6 0.8 stack.35
  1.4 1.3 fusion.2.small
  2.7 40.0 %gather.1 = (bf16[384,1152]{1,0:T(8,128)(2,1)}, bf16[384,384]{1,0:T(8,128)(2,1)}, bf16[384,1536]{1,0:T(8,128)(2,1)}, bf16[1536,384]{1,0:T(8,128)(2,1)}, f32[8,38...) custom-call(bf16[16,128]{1,0:T(8,128)(2,1)} %fusion.2.small, ...), custom_call_target="tpu_custom_call" | custom-call | tf_op jit(solution)/shard_map/gather/pallas_call | solution.py:652
  42.7 103.4 %middle.1 = (bf16[3072,384]{1,0:T(8,128)(2,1)}, f32[3072,384]{1,0:T(8,128)}, bf16[32,16,1024]{2,1,0:T(8,128)(2,1)}, bf16[32,16,2688]{2,1,0:T(8,128)(2,1)}) custom-call(s32[3072]{0:T(1024)} %start_in.1, s32[3072]{0:T(1024)} %end_in.1, bf16[3072,1152]{1,0:T(8,128)(2,1)} %get-tuple-element.44.qkv_in, bf16[272,1152]{1,0:T(8,128)(2,1)} %get-tuple-element.45.qkvh_in, ...), custom_call_target="tpu_custom_call" | custom-call | tf_op jit(solution)/shard_map/middle/pallas_call | solution.py:398
  146.1 33.8 %scatter.1 = (f32[16,1024]{1,0:T(8,128)}, f32[16,2688]{1,0:T(8,128)}) custom-call(bf16[32,16,1024]{2,1,0:T(8,128)(2,1)} %get-tuple-element.56.first_in, bf16[32,16,2688]{2,1,0:T(8,128)(2,1)} %get-tuple-element.57.second_in), custom_call_target="tpu_custom_call" | custom-call | tf_op jit(solution)/shard_map/scatter/pallas_call | solution.py:855
  179.9 1.7 finish.1

commit v4 on v3

--- a/solution.py
+++ b/solution.py
@@ -20,6 +20,7 @@
 HALO = LEFT + RIGHT
 KEYS = 224
 WIN = 256
+AHEAD = 4
 SPARE = 64
 SHORTEST, LONGEST = 98, 197
 AXES = ("dp", "fsdp")
@@ -94,10 +95,11 @@
     return s, e, a
 
 
-def put(ref, a, columns, value, first_row, old):
+def put(ref, a, columns, value, first_row):
     rows = value.shape[0]
+    old = ref[pl.ds(a, 16), columns].astype(F32)
     row = lax.broadcasted_iota(jnp.int32, (16, value.shape[1]), 0) + a
-    ref[pl.ds(a, 16), columns] = jnp.where(row >= first_row, value[:16].astype(F32), old[:, columns].astype(F32)).astype(ref.dtype)
+    ref[pl.ds(a, 16), columns] = jnp.where(row >= first_row, value[:16].astype(F32), old).astype(ref.dtype)
     ref[pl.ds(a + 16, rows - 16), columns] = value[16:].astype(ref.dtype)
 
 
@@ -107,73 +109,93 @@
     return low.astype(BF16), (1.0 - low).astype(BF16)
 
 
-def attention_forward(i, starts, ends, qkv, probs, att, width):
-    s, e, a = image_bounds(i, starts, ends)
-    row = lax.broadcasted_iota(jnp.int32, (KEYS, 1), 0) + a
-    inside = (row >= s) & (row < e)
-    key_bias = jnp.where(inside, 0.0, NEG)
-    col = lax.broadcasted_iota(jnp.int32, (1, WIN), 1) + a
-    query_on = jnp.where((col >= s) & (col < e), 1.0, 0.0)
+def attention_forward(images, starts, ends, qkv, probs, att, width):
     masks = lane_masks(KEYS)
-    old_probs, old_att = probs[pl.ds(a, 16), :], att[pl.ds(a, 16), :]
-    for pair in range(width // 128):
-        lanes = slice(128 * pair, 128 * pair + 128)
-        q = qkv[pl.ds(a, WIN), lanes]
+    sides = []
+    for i in images:
+        s, e, a = image_bounds(i, starts, ends)
+        row = lax.broadcasted_iota(jnp.int32, (KEYS, 1), 0) + a
+        key_bias = jnp.where((row >= s) & (row < e), 0.0, NEG)
+        col = lax.broadcasted_iota(jnp.int32, (1, WIN), 1) + a
+        query_on = jnp.where((col >= s) & (col < e), 1.0, 0.0)
+        sides.append((s, a, key_bias, query_on))
+
+    def scores_of(image, head):
+        s, a, key_bias, _ = sides[image]
+        pair, half = divmod(head, 2)
+        q = qkv[pl.ds(a, WIN), 128 * pair : 128 * pair + 128]
         k = qkv[pl.ds(a, KEYS), width + 128 * pair : width + 128 * pair + 128]
+        return dot_nt(k * masks[half], q)
+
+    steps = [(image, 2 * pair + half) for pair in range(width // 128) for half in range(2) for image in range(len(images))]
+    ready = [scores_of(*step) for step in steps[:AHEAD]]
+    total = [None] * len(images)
+    for n, (image, head) in enumerate(steps):
+        s, a, key_bias, query_on = sides[image]
+        pair, half = divmod(head, 2)
+        if n + AHEAD < len(steps):
+            ready.append(scores_of(*steps[n + AHEAD]))
+        scores = ready[n]
+        scores = jnp.concatenate([scores[:16] + key_bias[:16], scores[16:96], scores[96:] + key_bias[96:]], axis=0)
+        top = jnp.max(scores, axis=0, keepdims=True)
+        ex = jnp.exp(scores - top)
+        p = (ex * (query_on / jnp.sum(ex, axis=0, keepdims=True))).astype(BF16)
+        put(probs, a, slice(WIN * head, WIN * head + WIN), p, s)
         v = qkv[pl.ds(a, KEYS), 2 * width + 128 * pair : 2 * width + 128 * pair + 128]
-        total = None
-        for half in range(2):
-            head = 2 * pair + half
-            scores = dot_nt(k * masks[half], q) + key_bias
-            top = jnp.max(scores, axis=0, keepdims=True)
-            ex = jnp.exp(scores - top)
-            p = (ex * (query_on / jnp.sum(ex, axis=0, keepdims=True))).astype(BF16)
-            put(probs, a, slice(WIN * head, WIN * head + WIN), p, s, old_probs)
-            part = dot_tn(p, v * masks[half])
-            total = part if total is None else total + part
-        put(att, a, lanes, total, s, old_att)
-
-
-def attention_backward(i, starts, ends, qkv, probs, att, datt, dqkv, gvec, width, rows):
-    s, e, a = image_bounds(i, starts, ends)
+        part = dot_tn(p, v * masks[half])
+        total[image] = part if half == 0 else total[image] + part
+        if half == 1:
+            put(att, a, slice(128 * pair, 128 * pair + 128), total[image], s)
+
+
+def attention_backward(images, fresh, starts, ends, qkv, probs, att, datt, dqkv, gvec, width, rows):
     scale = 1.0 / math.sqrt(HDIM)
-    row = lax.broadcasted_iota(jnp.int32, (KEYS, 128), 0) + a
-    inside = jnp.where((row >= s) & (row < e), 1.0, 0.0).astype(BF16)
-    key_masks = [m * inside for m in lane_masks(KEYS)]
-    masks = lane_masks(KEYS)
-    wide_masks = lane_masks(WIN)
-    query = lax.broadcasted_iota(jnp.int32, (WIN, 128), 0) + a
-    own = jnp.where((query >= LEFT) & (query < LEFT + rows), 1.0, 0.0)
+    masks, wide_masks = lane_masks(KEYS), lane_masks(WIN)
     group = lax.broadcasted_iota(jnp.int32, (8, width), 1) // HDIM
     heads = jnp.where(group == lax.broadcasted_iota(jnp.int32, (8, width), 0), 1.0, 0.0).astype(BF16)
-    both = att[pl.ds(a, WIN), :].astype(F32) * datt[pl.ds(a, WIN), :].astype(F32)
-    high = both.astype(BF16)
-    old = dqkv[pl.ds(a, 16), :]
-    delta = dot_nt(heads, high) + dot_nt(heads, (both - high.astype(F32)).astype(BF16))
-    for pair in range(width // 128):
+    sides = []
+    for i, on in zip(images, fresh):
+        s, e, a = image_bounds(i, starts, ends)
+        row = lax.broadcasted_iota(jnp.int32, (KEYS, 128), 0) + a
+        inside = jnp.where((row >= s) & (row < e), 1.0, 0.0).astype(BF16)
+        query = lax.broadcasted_iota(jnp.int32, (WIN, 128), 0) + a
+        own = jnp.where((query >= LEFT) & (query < LEFT + rows), on, 0.0)
+        both = att[pl.ds(a, WIN), :].astype(F32) * datt[pl.ds(a, WIN), :].astype(F32)
+        high = both.astype(BF16)
+        delta = dot_nt(heads, high) + dot_nt(heads, (both - high.astype(F32)).astype(BF16))
+        sides.append((s, a, inside, own, delta))
+
+    def dprobs_of(image, head):
+        s, a, _, _, _ = sides[image]
+        pair, half = divmod(head, 2)
+        v = qkv[pl.ds(a, KEYS), 2 * width + 128 * pair : 2 * width + 128 * pair + 128]
+        return dot_nt(v * masks[half], datt[pl.ds(a, WIN), 128 * pair : 128 * pair + 128])
+
+    steps = [(image, 2 * pair + half) for pair in range(width // 128) for half in range(2) for image in range(len(images))]
+    ready = [dprobs_of(*step) for step in steps[:AHEAD]]
+    sums = [None] * len(images)
+    for n, (image, head) in enumerate(steps):
+        s, a, inside, own, delta = sides[image]
+        pair, half = divmod(head, 2)
+        if n + AHEAD < len(steps):
+            ready.append(dprobs_of(*steps[n + AHEAD]))
         lanes = slice(128 * pair, 128 * pair + 128)
         klanes = slice(width + 128 * pair, width + 128 * pair + 128)
         vlanes = slice(2 * width + 128 * pair, 2 * width + 128 * pair + 128)
-        q = qkv[pl.ds(a, WIN), lanes]
-        k = qkv[pl.ds(a, KEYS), klanes]
-        v = qkv[pl.ds(a, KEYS), vlanes]
-        do = datt[pl.ds(a, WIN), lanes]
-        dq = dk = dv = None
-        for half in range(2):
-            head = 2 * pair + half
-            p = probs[pl.ds(a, KEYS), WIN * head : WIN * head + WIN]
-            dp = dot_nt(v * masks[half], do)
-            ds = (p.astype(F32) * (dp - delta[head : head + 1])).astype(BF16)
-            dv_part = dot(p, do * wide_masks[half])
-            dk_part = dot(ds, q * wide_masks[half])
-            dq_part = dot_tn(ds, k * key_masks[half])
-            dv = dv_part if dv is None else dv + dv_part
-            dk = dk_part if dk is None else dk + dk_part
-            dq = dq_part if dq is None else dq + dq_part
-        gvec[0:1, lanes] += colsum(dq * own) * scale
-        put(dqkv, a, lanes, dq * scale, s, old)
-        put(dqkv, a, klanes, dk, s, old)
-        put(dqkv, a, vlanes, dv, s, old)
+        p = probs[pl.ds(a, KEYS), WIN * head : WIN * head + WIN]
+        ds = (p.astype(F32) * (ready[n] - delta[head : head + 1])).astype(BF16)
+        parts = (
+            dot_tn(ds, qkv[pl.ds(a, KEYS), klanes] * (inside * masks[half])),
+            dot(ds, qkv[pl.ds(a, WIN), lanes] * wide_masks[half]),
+            dot(p, datt[pl.ds(a, WIN), lanes] * wide_masks[half]),
+        )
+        sums[image] = parts if half == 0 else tuple(x + y for x, y in zip(sums[image], parts))
+        if half == 1:
+            dq, dk, dv = sums[image]
+            gvec[0:1, lanes] += colsum(dq * own) * scale
+            put(dqkv, a, lanes, dq * scale, s)
+            put(dqkv, a, klanes, dk, s)
+            put(dqkv, a, vlanes, dv, s)
 
 
 def middle_kernel(
@@ -234,14 +256,14 @@
 
     assert 3 * LONGEST + WIN <= early and rows > 5 * LONGEST
 
-    @pl.loop(0, count)
+    @pl.loop(0, (count + 1) // 2)
     def _(i):
-        @pl.when(i == 4)
+        @pl.when(i == 2)
         def _():
             for c in rest:
                 c.wait()
 
-        attention_forward(i, starts, ends, qkv, probs, att, width)
+        attention_forward([2 * i, jnp.minimum(2 * i + 1, count - 1)], starts, ends, qkv, probs, att, width)
 
     bo, bd, g1, b1, g2, b2 = (vec[j : j + 1, :] for j in (2, 3, 4, 5, 6, 7))
 
@@ -338,9 +360,9 @@
     row_read(0).start()
     gw[...] = jnp.zeros(gw.shape, F32)
 
-    @pl.loop(0, count)
+    @pl.loop(0, (count + 1) // 2)
     def _(i):
-        attention_backward(i, starts, ends, qkv, probs, att, datt, dqkv, gsum, width, rows)
+        attention_backward([2 * i, jnp.minimum(2 * i + 1, count - 1)], [1.0, jnp.where(2 * i + 1 < count, 1.0, 0.0)], starts, ends, qkv, probs, att, datt, dqkv, gsum, width, rows)
 
     @pl.loop(0, tiles)
     def _(i):

time: 182 us -> 173 us (0.951)
  Pallas kernels: 179 us -> 170 us
    pallas_call x1, Pallas kernels: 103 us -> 94.4 us  [middle(): pl.pallas_call(functools.partial(middle_kernel, packs), out_shape=[S((row...]
where the time goes in v4:
time: 173 us
  Pallas kernels  170 us (98%)
    pallas_call x1, Pallas kernels, middle(): pl.pallas_call(functools.partial(middle_kernel, packs), out_shape=[S((row...  94.4 us
    pallas_call x1, Pallas kernels, gather_all(): pl.pallas_call(gather_kernel, out_shape=(S((width, wqkv.shape[1]), BF16),...  40 us
    pallas_call x1, Pallas kernels, scatter_all(): pl.pallas_call(scatter_kernel, out_shape=(S((16, FIRST), F32), S((16, SEC...  33.8 us

profile of v4, /device:TPU:0, one launch (start us, length us, event | category | flops | bytes accessed | tf_op | source)
XLA Modules:
  0.0 172.8 jit_solution(1510112823180652472)
XLA Ops:
  0.6 0.8 stack.35
  1.4 1.3 fusion.2.small
  2.7 40.0 %gather.1 = (bf16[384,1152]{1,0:T(8,128)(2,1)}, bf16[384,384]{1,0:T(8,128)(2,1)}, bf16[384,1536]{1,0:T(8,128)(2,1)}, bf16[1536,384]{1,0:T(8,128)(2,1)}, f32[8,38...) custom-call(bf16[16,128]{1,0:T(8,128)(2,1)} %fusion.2.small, ...), custom_call_target="tpu_custom_call" | custom-call | tf_op jit(solution)/shard_map/gather/pallas_call | solution.py:674
  42.7 94.4 %middle.1 = (bf16[3072,384]{1,0:T(8,128)(2,1)}, f32[3072,384]{1,0:T(8,128)}, bf16[32,16,1024]{2,1,0:T(8,128)(2,1)}, bf16[32,16,2688]{2,1,0:T(8,128)(2,1)}) custom-call(s32[3072]{0:T(1024)} %start_in.1, s32[3072]{0:T(1024)} %end_in.1, bf16[3072,1152]{1,0:T(8,128)(2,1)} %get-tuple-element.44.qkv_in, bf16[272,1152]{1,0:T(8,128)(2,1)} %get-tuple-element.45.qkvh_in, ...), custom_call_target="tpu_custom_call" | custom-call | tf_op jit(solution)/shard_map/middle/pallas_call | solution.py:420
  137.1 33.8 %scatter.1 = (f32[16,1024]{1,0:T(8,128)}, f32[16,2688]{1,0:T(8,128)}) custom-call(bf16[32,16,1024]{2,1,0:T(8,128)(2,1)} %get-tuple-element.56.first_in, bf16[32,16,2688]{2,1,0:T(8,128)(2,1)} %get-tuple-element.57.second_in), custom_call_target="tpu_custom_call" | custom-call | tf_op jit(solution)/shard_map/scatter/pallas_call | solution.py:877
  170.9 1.7 finish.1
